TPU v7x, 256 devices: a whole 4x4x8 slice. The times are simulated.
256 devices in a mesh: sa: 32 (over z_lo, x, core), sb: 8 (over z_hi, y).
Axes of the slice: x: 4, y: 4, z: 8 (z_hi: 2, z_lo: 4; z = z_hi * 4 + z_lo), core: 2. Of those that a mesh axis runs over, the one named last changes fastest.
Arguments:
- tokens: bfloat16 [64, 32, 32, 2048], P('sa', 'sb'), may hold values from -6 to 6
- norm_gain: float32 [2048], replicated, may hold values from 0.5 to 1.5
- gate_weight: bfloat16 [2048, 2048], P(('sa', 'sb')), may hold values from -0.125 to 0.125
- level_one: bfloat16 [32, 32, 64, 64], P('sb', 'sa'), may hold values from -0.75 to 0.75
- level_two: bfloat16 [64, 32, 32, 32], P('sa', 'sb'), may hold values from -1 to 1
- level_three: bfloat16 [64, 32, 32, 32], P('sa', 'sb'), may hold values from -1 to 1
- upstream: bfloat16 [64, 32, 32, 2048], P('sa', 'sb'), may hold values from -6 to 6
Outputs:
- output: bfloat16 [64, 32, 32, 2048], P('sa', 'sb')
- grad_tokens: bfloat16 [64, 32, 32, 2048], P('sa', 'sb')
- grad_one: float32 [32, 32, 64, 64], P('sb', 'sa')
- grad_two: float32 [64, 32, 32, 32], P('sa', 'sb')
- grad_three: float32 [64, 32, 32, 32], P('sa', 'sb')
All inputs are finite; a program needn't handle non-finite values.
Results may differ from a plain program's by a relative error of at most 0.0071.
Values may be sent and summed in bfloat16 or wider, within the bound.
A program may use at most 128 MiB of HBM per device.

v0:
```python
import functools

import jax
import jax.numpy as jnp
from jax import lax
from jax.experimental import pallas as pl
from jax.experimental.pallas import tpu as pltpu
from jax.sharding import PartitionSpec as P

ALL = ("sa", "sb")
EPSILON = 1e-06


MESH = pl.DeviceIdType.MESH


def pack_blocks(values):
    i, j, k, c = values.shape
    sa, sb = lax.axis_size("sa"), lax.axis_size("sb")
    parts = values.reshape(i, j, sa, sb, c // sb).transpose(2, 3, 0, 1, 4)
    return parts.reshape(sa * sb, i * j, c // sb)


def unpack_blocks(parts, i, j):
    sa, sb = lax.axis_size("sa"), lax.axis_size("sb")
    c = parts.shape[2]
    parts = parts.reshape(sa, sb, i, j, c).transpose(0, 2, 1, 3, 4)
    return parts.reshape(sa * i, sb * j, c)


def pack_tokens(values):
    sa, sb = lax.axis_size("sa"), lax.axis_size("sb")
    i, j, c = values.shape[0] // sa, values.shape[1] // sb, values.shape[2]
    parts = values.reshape(sa, i, sb, j, c).transpose(0, 2, 1, 3, 4)
    return parts.reshape(sa * sb, i * j, c)


def unpack_tokens(parts, i, j):
    sa, sb = lax.axis_size("sa"), lax.axis_size("sb")
    c = parts.shape[2]
    parts = parts.reshape(sa, sb, i, j, c).transpose(2, 3, 0, 1, 4)
    return parts.reshape(i, j, sa, sb * c)


def exchange(parts):
    return lax.all_to_all(parts, ALL, split_axis=0, concat_axis=0, tiled=True)


def signal_all(peers):
    barrier = pltpu.get_barrier_semaphore()
    for peer in peers:
        pl.semaphore_signal(barrier, inc=1, device_id=peer, device_id_type=MESH)
    return barrier


def remote(source, target, send, recv, peer):
    return pltpu.make_async_remote_copy(
        src_ref=source,
        dst_ref=target,
        send_sem=send,
        recv_sem=recv,
        device_id=peer,
        device_id_type=MESH,
    )


def gather_kernel(low_column, width, with_levels, *refs):
    if with_levels:
        (w_ref, one_ref, two_ref, out_ref, all_one, all_two, own_sem, send, recv,
         level_own, level_send, level_recv) = refs
    else:
        w_ref, _, out_ref, own_sem, send, recv = refs
    sa, sb = lax.axis_index("sa"), lax.axis_index("sb")
    z_lo, x, core = sa // 8, (sa // 2) % 4, sa % 2
    z_hi, y = sb // 4, sb % 4
    z = z_hi * 4 + z_lo

    def at(z_at, x_at, y_at, core_at):
        return ((z_at % 4) * 8 + x_at * 2 + core_at, (z_at // 4) * 4 + y_at)

    along_z = [at((z + d) % 8, x, y, core) for d in range(1, 8)]
    step_x = [at(z, (x + d) % 4, y, core) for d in (1, 3)]
    step_y = [at(z, x, (y + d) % 4, core) for d in (1, 3)]
    partner = at(z, x, y, 1 - core)
    along_sb = [(sa, (sb + d) % 8) for d in range(1, 8)]
    greeted = along_z + step_x + step_y + [partner]
    barrier = signal_all(greeted + (along_sb if with_levels else []))
    if with_levels:
        source_sb = sa // 4

        def greet(n, carry):
            @pl.when(jnp.logical_or(n != sa, source_sb != sb))
            def _():
                pl.semaphore_signal(
                    barrier, inc=1, device_id=(n, source_sb), device_id_type=MESH
                )

            return carry

        lax.fori_loop(0, 32, greet, 0)
        outside = jnp.where(source_sb != sb, 1, 0)
        pl.semaphore_wait(barrier, len(greeted) + 7 + 31 + outside)
    else:
        pl.semaphore_wait(barrier, len(greeted))

    started = []

    def push(source, target, peer):
        n = len(started)
        copy = remote(source, target, send.at[n], recv.at[n], peer)
        copy.start()
        started.append(copy)
        return copy

    shared = []

    def share(piece):
        shared.append(push(piece, piece, partner))

    every = pl.ds(low_column, width)
    own = out_ref.at[z_lo, x, core, z_hi, y, :, every]
    keep = pltpu.make_async_copy(w_ref.at[:, every], own, own_sem)
    keep.start()
    first = [push(w_ref.at[:, every], own, peer) for peer in along_z]

    if with_levels:
        ones = []
        keep_one = pltpu.make_async_copy(one_ref, all_one.at[sb], level_own.at[0])
        keep_one.start()
        for d, peer in enumerate(along_sb):
            copy = remote(
                one_ref, all_one.at[sb], level_send.at[32 + d], level_recv.at[32 + d], peer
            )
            copy.start()
            ones.append(copy)

        def two_copy(n):
            return remote(
                two_ref.at[:, n // 8],
                all_two.at[sa],
                level_send.at[n],
                level_recv.at[sa],
                (4 * sb + n // 8, n % 8),
            )

        def is_self(n):
            return jnp.logical_and(4 * sb + n // 8 == sa, n % 8 == sb)

        def send_two(n, carry):
            @pl.when(jnp.logical_not(is_self(n)))
            def _():
                two_copy(n).start()

            @pl.when(is_self(n))
            def _():
                pltpu.make_async_copy(
                    two_ref.at[:, n // 8], all_two.at[sa], level_own.at[1]
                ).start()

            return carry

        lax.fori_loop(0, 32, send_two, 0)

    keep.wait()
    for copy in first:
        copy.wait_recv()

    half, quarter = width // 2, width // 4

    def piece_x(stage, at_x, low, size):
        if stage == 0:
            return out_ref.at[:, at_x, core, :, y, :, pl.ds(low, size)]
        return out_ref.at[:, at_x, core, :, :, :, pl.ds(low, size)]

    def piece_y(stage, at_y, low, size):
        if stage == 0:
            return out_ref.at[:, x, core, :, at_y, :, pl.ds(low, size)]
        return out_ref.at[:, :, core, :, at_y, :, pl.ds(low, size)]

    streams = (
        (low_column, ((piece_x, x, step_x), (piece_y, y, step_y))),
        (low_column + half, ((piece_y, y, step_y), (piece_x, x, step_x))),
    )
    for stage in range(2):
        opened = []
        for low, orders in streams:
            piece, here, peers = orders[stage]
            mine = piece(stage, here, low, half)
            opened.append([push(mine, mine, peer) for peer in peers])
        if stage == 0:
            share(out_ref.at[:, x, core, :, y, :, every])
        passed = []
        for (low, orders), (up, down) in zip(streams, opened):
            piece, here, peers = orders[stage]
            below, above = (here + 3) % 4, (here + 1) % 4
            up.wait_recv()
            onward = piece(stage, below, low, quarter)
            one = push(onward, onward, peers[0])
            share(piece(stage, below, low, half))
            down.wait_recv()
            onward = piece(stage, above, low + quarter, quarter)
            other = push(onward, onward, peers[1])
            share(piece(stage, above, low, half))
            passed.append((one, other))
        for (low, orders), (one, other) in zip(streams, passed):
            piece, here, peers = orders[stage]
            one.wait_recv()
            other.wait_recv()
            share(piece(stage, (here + 2) % 4, low, half))
    for copy in shared:
        copy.wait_recv()
    for copy in started:
        copy.wait_send()

    if with_levels:
        keep_one.wait()
        for copy in ones:
            copy.wait()

        def wait_two(n, carry):
            @pl.when(jnp.logical_not(is_self(n)))
            def _():
                two_copy(n).wait_send()

            @pl.when(is_self(n))
            def _():
                pltpu.make_async_copy(
                    two_ref.at[:, n // 8], all_two.at[sa], level_own.at[1]
                ).wait()

            @pl.when(jnp.logical_or(n != sa, source_sb != sb))
            def _():
                remote(
                    two_ref.at[:, 0],
                    all_two.at[n],
                    level_send.at[n],
                    level_recv.at[n],
                    (n, source_sb),
                ).wait_recv()

            return carry

        lax.fori_loop(0, 32, wait_two, 0)


GATHER_COPIES = 7 + 16 + 13


def gather_first(weight, level_one, level_two, width):
    rows, columns = weight.shape
    whole = pl.BlockSpec(memory_space=pltpu.VMEM)
    dma = pltpu.SemaphoreType.DMA
    return pl.pallas_call(
        functools.partial(gather_kernel, 0, width, True),
        out_shape=(
            jax.ShapeDtypeStruct((4, 4, 2, 2, 4, rows, columns), weight.dtype),
            jax.ShapeDtypeStruct((8, *level_one.shape), level_one.dtype),
            jax.ShapeDtypeStruct((32, level_two.shape[0], *level_two.shape[2:]), level_two.dtype),
        ),
        in_specs=[whole] * 3,
        out_specs=(pl.BlockSpec(memory_space=pl.ANY), whole, whole),
        scratch_shapes=[
            dma(()), dma((GATHER_COPIES,)), dma((GATHER_COPIES,)),
            dma((2,)), dma((39,)), dma((39,)),
        ],
        compiler_params=pltpu.CompilerParams(collective_id=0, has_side_effects=True),
        cost_estimate=pl.CostEstimate(
            flops=10**9, bytes_accessed=8 * rows * columns * 256, transcendentals=0
        ),
        name="gather_first",
    )(weight, level_one, level_two)


def gather_rest(weight, gathered, low):
    rows, columns = weight.shape
    dma = pltpu.SemaphoreType.DMA
    return pl.pallas_call(
        functools.partial(gather_kernel, low, columns - low, False),
        out_shape=jax.ShapeDtypeStruct(gathered.shape, gathered.dtype),
        in_specs=[pl.BlockSpec(memory_space=pltpu.VMEM), pl.BlockSpec(memory_space=pl.ANY)],
        out_specs=pl.BlockSpec(memory_space=pl.ANY),
        input_output_aliases={1: 0},
        scratch_shapes=[dma(()), dma((GATHER_COPIES,)), dma((GATHER_COPIES,))],
        compiler_params=pltpu.CompilerParams(collective_id=1, has_side_effects=True),
        cost_estimate=pl.CostEstimate(
            flops=10**9, bytes_accessed=8 * rows * columns * 256, transcendentals=0
        ),
        name="gather_rest",
    )(weight, gathered)


def reduce_kernel(scale, one_ref, two_ref, sum_one, sum_two, got_one, got_two, send, recv):
    sa, sb = lax.axis_index("sa"), lax.axis_index("sb")
    along_sb = [(sa, (sb + d) % 8) for d in range(1, 8)]
    barrier = signal_all(along_sb)
    target_sb = sa // 4

    def is_self(n):
        return jnp.logical_and(4 * sb + n // 8 == sa, n % 8 == sb)

    def greet(n, carry):
        @pl.when(jnp.logical_not(is_self(n)))
        def _():
            pl.semaphore_signal(
                barrier, inc=1, device_id=(4 * sb + n // 8, n % 8), device_id_type=MESH
            )

        return carry

    lax.fori_loop(0, 32, greet, 0)
    pl.semaphore_wait(barrier, 7 + 31 + jnp.where(target_sb != sb, 1, 0))

    ones = []
    for d in range(7):
        to = (sb + d + 1) % 8
        copy = remote(
            one_ref.at[to], got_one.at[sb], send.at[32 + d], recv.at[32 + d], (sa, to)
        )
        copy.start()
        ones.append(copy)

    mine = (sa % 4) * 8 + sb

    def goes_out(n):
        return jnp.logical_or(n != sa, target_sb != sb)

    def two_copy(n):
        return remote(
            two_ref.at[n], got_two.at[mine], send.at[n], recv.at[mine], (n, target_sb)
        )

    def send_two(n, carry):
        @pl.when(goes_out(n))
        def _():
            two_copy(n).start()

        return carry

    lax.fori_loop(0, 32, send_two, 0)

    @pl.when(target_sb == sb)
    def _():
        got_two[mine] = two_ref[sa]

    got_one[sb] = one_ref[sb]

    def wait_two(n, carry):
        @pl.when(goes_out(n))
        def _():
            two_copy(n).wait_send()

        @pl.when(jnp.logical_not(is_self(n)))
        def _():
            remote(
                two_ref.at[0],
                got_two.at[n],
                send.at[n],
                recv.at[n],
                (4 * sb + n // 8, n % 8),
            ).wait_recv()

        return carry

    lax.fori_loop(0, 32, wait_two, 0)
    for copy in ones:
        copy.wait()
    total = got_one[0].astype(jnp.float32)
    for n in range(1, 8):
        total += got_one[n].astype(jnp.float32)
    sum_one[...] = total * scale
    for k in range(4):
        total = got_two[8 * k].astype(jnp.float32)
        for n in range(1, 8):
            total += got_two[8 * k + n].astype(jnp.float32)
        sum_two[k] = total * scale


def reduce_parts(part_one, part_two, scale):
    dma = pltpu.SemaphoreType.DMA
    whole = pl.BlockSpec(memory_space=pltpu.VMEM)
    return pl.pallas_call(
        functools.partial(reduce_kernel, scale),
        out_shape=(
            jax.ShapeDtypeStruct(part_one.shape[1:], jnp.float32),
            jax.ShapeDtypeStruct((4, *part_two.shape[1:]), jnp.float32),
        ),
        in_specs=[whole] * 2,
        out_specs=(whole, whole),
        scratch_shapes=[
            pltpu.VMEM(part_one.shape, part_one.dtype),
            pltpu.VMEM(part_two.shape, part_two.dtype),
            dma((39,)),
            dma((39,)),
        ],
        compiler_params=pltpu.CompilerParams(collective_id=2, has_side_effects=True),
        cost_estimate=pl.CostEstimate(flops=10**8, bytes_accessed=2**20, transcendentals=0),
        name="reduce_parts",
    )(part_one, part_two)


def dot(pattern, left, right):
    return jnp.einsum(pattern, left, right, preferred_element_type=jnp.float32)


def body(tokens, norm_gain, gate_weight, level_one, level_two, level_three, upstream):
    own_i, own_j, own_k, channels = tokens.shape
    sa, sb = lax.axis_size("sa"), lax.axis_size("sb")
    m1, m2 = level_one.shape[2], level_two.shape[2]
    grad_scale = channels ** (-0.5)
    after = lax.optimization_barrier

    tokens_float = tokens.astype(jnp.float32)
    inverse_rms = lax.rsqrt(jnp.mean(tokens_float * tokens_float, axis=3, keepdims=True) + EPSILON)
    normed = (tokens_float * inverse_rms * norm_gain).astype(jnp.bfloat16)

    parts, weight_late = after((pack_blocks(normed), gate_weight))
    normed_block = exchange(parts)
    gathered, block_one, block_two = gather_first(
        weight_late,
        level_one.reshape(own_j, -1, 128),
        level_two.reshape(own_i, level_two.shape[1], -1, 128),
        channels // 2,
    )
    block_one = block_one.reshape(sb * own_j, m1, m1)
    block_two = block_two.reshape(sa * own_i, m2, m2)

    normed_block = unpack_blocks(normed_block, own_i, own_j)
    first_mix = dot("joi,ijc->ojc", block_one, normed_block).astype(jnp.bfloat16)
    second_mix = dot("ioj,ijc->ioc", block_two, first_mix).astype(jnp.bfloat16)
    parts, weight_late, gathered = after((pack_tokens(second_mix), gate_weight, gathered))
    second_mix = exchange(parts)
    gathered = gather_rest(weight_late, gathered, channels // 2).reshape(-1, channels)
    gate_pre = dot("tr,rc->tc", normed.reshape(-1, channels), gathered).reshape(tokens.shape)
    gate_pre, second_mix = after((gate_pre, second_mix))
    second_mix = unpack_tokens(second_mix, own_i, own_j)
    mixed_all = dot("ijok,ijkc->ijoc", level_three, second_mix)

    gate_sigmoid = jax.nn.sigmoid(gate_pre)
    gate_value = gate_pre * gate_sigmoid
    output = (tokens_float + mixed_all * gate_value).astype(jnp.bfloat16)
    upstream_float = upstream.astype(jnp.float32)
    grad_mixed = (upstream_float * gate_value).astype(jnp.bfloat16)
    grad_gate = (
        upstream_float * mixed_all * gate_sigmoid * (1.0 + gate_pre * (1.0 - gate_sigmoid))
    ).astype(jnp.bfloat16)
    grad_second = dot("ijok,ijoc->ijkc", level_three, grad_mixed).astype(jnp.bfloat16)

    parts, grad_gate, grad_mixed = after((pack_blocks(grad_second), grad_gate, grad_mixed))
    grad_block = exchange(parts)
    back_term = dot("tc,rc->tr", grad_gate.reshape(-1, channels), gathered)
    grad_three = dot("ijoc,ijkc->ijok", grad_mixed, second_mix) * grad_scale
    grad_block, back_term, grad_three = after((grad_block, back_term, grad_three))

    grad_block = unpack_blocks(grad_block, own_i, own_j)
    grad_first = dot("ioj,ioc->ijc", block_two, grad_block).astype(jnp.bfloat16)
    grad_normed = dot("joi,ojc->ijc", block_one, grad_first).astype(jnp.bfloat16)
    parts, grad_block, grad_first = after((pack_tokens(grad_normed), grad_block, grad_first))
    grad_normed = exchange(parts)
    part_two = dot("ioc,ijc->ioj", grad_block, first_mix).astype(jnp.bfloat16)
    part_one = dot("ojc,ijc->joi", grad_first, normed_block).astype(jnp.bfloat16)
    grad_one, grad_two = reduce_parts(
        part_one.reshape(sb, -1, 128), part_two.reshape(sa, own_i, -1, 128), grad_scale
    )
    grad_normed, grad_one, grad_two = after((grad_normed, grad_one, grad_two))
    grad_one = grad_one.reshape(level_one.shape)
    grad_two = grad_two.transpose(1, 0, 2, 3).reshape(level_two.shape)

    grad_normed = unpack_tokens(grad_normed, own_i, own_j)
    grad_hidden = grad_normed.astype(jnp.float32) + back_term.reshape(tokens.shape)
    weighted = grad_hidden * norm_gain
    average = jnp.mean(weighted * tokens_float, axis=3, keepdims=True)
    grad_tokens = (
        upstream_float + inverse_rms * weighted - tokens_float * inverse_rms**3 * average
    ).astype(jnp.bfloat16)
    return (output, grad_tokens, grad_one, grad_two, grad_three)


def solution(mesh):
    token_spec = P("sa", "sb", None, None)
    block_spec = P("sb", "sa", None, None)
    in_specs = (token_spec, P(), P(ALL, None), block_spec, token_spec, token_spec, token_spec)
    out_specs = (token_spec, token_spec, block_spec, token_spec, token_spec)
    return jax.shard_map(body, mesh=mesh, in_specs=in_specs, out_specs=out_specs, check_vma=False)
```

profile of v0, /device:TPU:9, one launch (start us, length us, event | category | flops | bytes accessed | tf_op | source)
XLA Modules:
  0.0 299.2 jit_solution(829275240424416861)
XLA Ops:
  5.6 14.9 %all-to-all-start = ((bf16[256,8,256]{2,1,0:T(8,128)(2,1)}), bf16[256,8,256]{2,1,0:T(8,128)(2,1)S(1)}, u32[]{:S(2)}, u32[]{:S(2)}) async-start(bf16[256,8,256]{2,1,0:T(8,128)(2,1)} %copy.72), calls=%async_computation | async-start | bytes 2097152 | tf_op jit(solution)/shard_map/all_to_all | solution.py:46
  22.0 60.5 %gather_first.1 = (bf16[4,4,2,2,4,8,2048]{6,5,4,3,2,1,0:T(8,128)(2,1)}, bf16[8,4,32,128]{3,2,1,0:T(8,128)(2,1)}, bf16[32,2,8,128]{3,2,1,0:T(8,128)(2,1)}) custom-call(bf16[8,2048]{1,0:T(8,128)(2,1)} %refs_0_.1, bf16[4,32,128]{2,1,0:T(8,128)(2,1)} %reshape.116.refs_1_, bf16[2,4,8,128]{3,2,1,0:T(8,128)(2,1)} %reshape.117.refs_2_), custom_call_target="tpu_custom_call" | custom-call | flops 1000000000 | bytes 33554432 | tf_op jit(solution)/shard_map/gather_first/pallas_call | solution.py:253
  85.2 2.1 copy.49
  90.9 2.2 reshape.122
  96.0 12.8 %all-to-all-start.1 = ((bf16[256,8,256]{2,1,0:T(8,128)(2,1)}), bf16[256,8,256]{2,1,0:T(8,128)(2,1)}, u32[]{:S(2)}, u32[]{:S(2)}) async-start(bf16[256,8,256]{2,1,0:T(8,128)(2,1)} %copy.52), calls=%async_computation.1 | async-start | bytes 2097152 | tf_op jit(solution)/shard_map/all_to_all | solution.py:46
  108.9 53.8 %gather_rest.1 = bf16[4,4,2,2,4,8,2048]{6,5,4,3,2,1,0:T(8,128)(2,1)} custom-call(bf16[8,2048]{1,0:T(8,128)(2,1)} %refs_0_.1, bf16[4,4,2,2,4,8,2048]{6,5,4,3,2,1,0:T(8,128)(2,1)} %get-tuple-element.35.refs_1_), custom_call_target="tpu_custom_call", output_to_operand_aliasing={{}: (1, {})} | custom-call | flops 1000000000 | bytes 33554432 | tf_op jit(solution)/shard_map/gather_rest/pallas_call | solution.py:277
  162.7 7.2 %fusion.19 = f32[2,4,32,2048]{3,2,1,0:T(8,128)} fusion(bf16[2,4,32,2048]{3,2,1,0:T(8,128)(2,1)S(1)} %copy-done.8, bf16[2048,2048,1,1]{1,0,3,2:T(8,128)(2,1)} %bitcast.90), kind=kOutput, calls=%fused_computation.41 | convolution fusion | flops 2147483648 | bytes 11534336 | tf_op jit(solution)/shard_map/tr,rc->tc/dot_general | solution.py:402
  169.9 2.1 reshape.125
  172.0 2.5 copy.53
  174.5 2.3 reshape.126
  176.9 5.1 %fusion.3 = (bf16[2,4,32,2048]{3,2,1,0:T(8,128)(2,1)}, bf16[2,4,32,2048]{3,2,1,0:T(8,128)(2,1)}, bf16[2,4,32,2048]{3,2,1,0:T(8,128)(2,1)S(1)}) fusion(bf16[2,4,32,2048]{3,2,1,0:T(8,128)(2,1)} %param.13, f32[2,4,32,2048]{3,2,1,0:T(8,128)} %fusion.19, bf16[2,4,32,2048]{3,2,1,0:T(8,128)(2,1)S(1)} %copy-done.1, bf16[2,4,32,32]{3,2,1,0:T(8,128)(2,1)S(1)} %copy-done, ...), kind=kOutput, calls=%fused_computation.13 | convolution fusion | flops 42991616 | bytes 8404992 | tf_op jit(solution)/shard_map/ijok,ijkc->ijoc/dot_general | solution.py:402
  184.6 8.5 %all-to-all-start.2 = ((bf16[256,8,256]{2,1,0:T(8,128)(2,1)}), bf16[256,8,256]{2,1,0:T(8,128)(2,1)}, u32[]{:S(2)}, u32[]{:S(2)}) async-start(bf16[256,8,256]{2,1,0:T(8,128)(2,1)} %copy.73), calls=%async_computation.2 | async-start | bytes 2097152 | tf_op jit(solution)/shard_map/all_to_all | solution.py:46
  193.1 2.7 convolution_multiply_fusion
  195.8 7.1 %fusion.20 = f32[256,2048]{1,0:T(8,128)} fusion(bf16[256,2048]{1,0:T(8,128)(2,1)S(1)} %bitcast.104, bf16[2048,2048]{1,0:T(8,128)(2,1)} %bitcast.91), kind=kOutput, calls=%fused_computation.42 | convolution fusion | flops 2147483648 | bytes 11534336 | tf_op jit(solution)/shard_map/tc,rc->tr/dot_general | solution.py:402
  202.9 20.0 %all-to-all-done.2 = bf16[256,8,256]{2,1,0:T(8,128)(2,1)} async-done(((bf16[256,8,256]{2,1,0:T(8,128)(2,1)}), bf16[256,8,256]{2,1,0:T(8,128)(2,1)}, u32[]{:S(2)}, u32[]{:S(2)}) %all-to-all-start.2) | async-done | bytes 1048608 | tf_op jit(solution)/shard_map/all_to_all | solution.py:46
  224.3 2.3 copy.57
  226.6 2.1 reshape.131
  233.5 2.2 reshape.132
  239.2 9.1 %all-to-all-start.3 = ((bf16[256,8,256]{2,1,0:T(8,128)(2,1)}), bf16[256,8,256]{2,1,0:T(8,128)(2,1)}, u32[]{:S(2)}, u32[]{:S(2)}) async-start(bf16[256,8,256]{2,1,0:T(8,128)(2,1)} %copy.62), calls=%async_computation.3 | async-start | bytes 2097152 | tf_op jit(solution)/shard_map/all_to_all | solution.py:46
  248.2 2.8 convolution_convert_fusion.5
  251.1 2.0 reshape.135.two_ref
  256.0 31.4 %reduce_parts.1 = (f32[128,128]{1,0:T(8,128)}, f32[4,2,8,128]{3,2,1,0:T(8,128)}) custom-call(bf16[8,128,128]{2,1,0:T(8,128)(2,1)} %reshape.134.one_ref, bf16[32,2,8,128]{3,2,1,0:T(8,128)(2,1)} %reshape.135.two_ref), custom_call_target="tpu_custom_call" | custom-call | flops 100000000 | bytes 1048576 | tf_op jit(solution)/shard_map/reduce_parts/pallas_call | solution.py:381
  290.5 2.8 copy.74
  295.1 2.2 fusion.11
  (64 shorter events, 37.6 us)
Async XLA Ops:
  0.6 176.2 %copy-start = (bf16[2,4,32,32]{3,2,1,0:T(8,128)(2,1)S(1)}, bf16[2,4,32,32]{3,2,1,0:T(8,128)(2,1)}, u32[]{:S(2)}) copy-start(bf16[2,4,32,32]{3,2,1,0:T(8,128)(2,1)} %param.12) | copy-start | bytes 49156
  3.7 1.9 copy-start.7
  4.1 16.5 %copy-start.12 = (bf16[2,4,32,32]{3,2,1,0:T(8,128)(2,1)S(1)}, bf16[2,4,32,32]{3,2,1,0:T(8,128)(2,1)}, u32[]{:S(2)}) copy-start(bf16[2,4,32,32]{3,2,1,0:T(8,128)(2,1)} %param.11) | copy-start | bytes 49156
  4.1 17.2 %copy-start.13 = (bf16[4,1,64,64]{3,2,1,0:T(8,128)(2,1)S(1)}, bf16[4,1,64,64]{3,2,1,0:T(8,128)(2,1)}, u32[]{:S(2)}) copy-start(bf16[4,1,64,64]{3,2,1,0:T(8,128)(2,1)} %param.10) | copy-start | bytes 98308
  5.6 79.4 %all-to-all-start = ((bf16[256,8,256]{2,1,0:T(8,128)(2,1)}), bf16[256,8,256]{2,1,0:T(8,128)(2,1)S(1)}, u32[]{:S(2)}, u32[]{:S(2)}) async-start(bf16[256,8,256]{2,1,0:T(8,128)(2,1)} %copy.72), calls=%async_computation | async-start | bytes 2097152 | tf_op jit(solution)/shard_map/all_to_all | solution.py:46
  83.6 5.6 %copy-start.4 = (bf16[64,32,32]{2,1,0:T(8,128)(2,1)}, bf16[64,32,32]{2,1,0:T(8,128)(2,1)S(1)}, u32[]{:S(2)}) copy-start(bf16[64,32,32]{2,1,0:T(8,128)(2,1)S(1)} %reshape.118) | copy-start | bytes 393220
  85.0 3.8 %copy-start.5 = (bf16[32,64,64]{2,1,0:T(8,128)(2,1)}, bf16[32,64,64]{2,1,0:T(8,128)(2,1)S(1)}, u32[]{:S(2)}) copy-start(bf16[32,64,64]{2,1,0:T(8,128)(2,1)S(1)} %reshape.121) | copy-start | bytes 786436
  96.0 73.9 %all-to-all-start.1 = ((bf16[256,8,256]{2,1,0:T(8,128)(2,1)}), bf16[256,8,256]{2,1,0:T(8,128)(2,1)}, u32[]{:S(2)}, u32[]{:S(2)}) async-start(bf16[256,8,256]{2,1,0:T(8,128)(2,1)} %copy.52), calls=%async_computation.1 | async-start | bytes 2097152 | tf_op jit(solution)/shard_map/all_to_all | solution.py:46
  108.9 53.9 %copy-start.8 = (bf16[2,4,32,2048]{3,2,1,0:T(8,128)(2,1)S(1)}, bf16[2,4,32,2048]{3,2,1,0:T(8,128)(2,1)}, u32[]{:S(2)}) copy-start(bf16[2,4,32,2048]{3,2,1,0:T(8,128)(2,1)} %copy-done.7) | copy-start | bytes 3145732
  172.0 4.8 %copy-start.1 = (bf16[2,4,32,2048]{3,2,1,0:T(8,128)(2,1)S(1)}, bf16[2,4,32,2048]{3,2,1,0:T(8,128)(2,1)}, u32[]{:S(2)}) copy-start(bf16[2,4,32,2048]{3,2,1,0:T(8,128)(2,1)} %param.7) | copy-start | bytes 3145732
  182.0 1.0 copy-start.9
  184.6 38.3 %all-to-all-start.2 = ((bf16[256,8,256]{2,1,0:T(8,128)(2,1)}), bf16[256,8,256]{2,1,0:T(8,128)(2,1)}, u32[]{:S(2)}, u32[]{:S(2)}) async-start(bf16[256,8,256]{2,1,0:T(8,128)(2,1)} %copy.73), calls=%async_computation.2 | async-start | bytes 2097152 | tf_op jit(solution)/shard_map/all_to_all | solution.py:46
  193.1 2.7 copy-start.14
  228.7 2.9 copy-start.6
  230.7 1.0 copy-start.2
  239.2 48.2 %all-to-all-start.3 = ((bf16[256,8,256]{2,1,0:T(8,128)(2,1)}), bf16[256,8,256]{2,1,0:T(8,128)(2,1)}, u32[]{:S(2)}, u32[]{:S(2)}) async-start(bf16[256,8,256]{2,1,0:T(8,128)(2,1)} %copy.62), calls=%async_computation.3 | async-start | bytes 2097152 | tf_op jit(solution)/shard_map/all_to_all | solution.py:46
  293.3 1.7 copy-start.11
  295.0 2.2 copy-start.3
  295.0 2.5 copy-start.10
where the time goes:
time: 300 us; the launch traced here: 299 us
  Pallas kernels  146 us (49%)
  local copies, waits for them, and re-layouts  47.1 us (16%)
  starting transfers between devices  45.3 us (15%)
  matrix products  33.3 us (11%)
  waiting for transfers between devices  20 us (7%)
  other arithmetic  6.99 us (2%)
    pallas_call x1, Pallas kernels, gather_first(): pl.pallas_call(functools.partial(gather_kernel, 0, width, True), out_shap...  60.5 us
    pallas_call x1, Pallas kernels, gather_rest(): pl.pallas_call(functools.partial(gather_kernel, low, columns - low, False...  53.8 us
    all_to_all x4, starting transfers between devices, exchange(): return lax.all_to_all(parts, ALL, split_axis=0, concat_axis=0, tiled=True)  45.3 us
    dot_general x11, matrix products, dot(): return jnp.einsum(pattern, left, right, preferred_element_type=jnp.float32)  33.3 us
    pallas_call x1, Pallas kernels, reduce_parts(): pl.pallas_call(functools.partial(reduce_kernel, scale), out_shape=(jax.Sh...  31.4 us
    all_to_all x4, waiting for transfers between devices, exchange(): return lax.all_to_all(parts, ALL, split_axis=0, concat_axis=0, tiled=True)  20 us
    reshape x4, local copies, waits for them, and re-layouts, pack_tokens(): parts = values.reshape(sa, i, sb, j, c).transpose(0, 2, 1, 3, 4)  7.57 us
  transfers between devices with their start and end apart: 4, of which 1 were waited for; matrix products, arithmetic and copies ran while one was open for 10% of the time, Pallas kernels for 49%

commit v1 on v0

--- a/solution.py
+++ b/solution.py
@@ -64,12 +64,35 @@
     )
 
 
+def gather_z_kernel(w_ref, out_ref, own_sem, send, recv):
+    sa, sb = lax.axis_index("sa"), lax.axis_index("sb")
+    z_lo, z_hi = sa // 8, sb // 4
+    z = z_hi * 4 + z_lo
+    own = out_ref.at[z_lo, (sa // 2) % 4, sa % 2, z_hi, sb % 4]
+    along_z = []
+    for d in range(1, 8):
+        to = (z + d) % 8
+        along_z.append(((to % 4) * 8 + sa % 8, (to // 4) * 4 + sb % 4))
+    barrier = signal_all(along_z)
+    pl.semaphore_wait(barrier, len(along_z))
+    keep = pltpu.make_async_copy(w_ref, own, own_sem)
+    keep.start()
+    copies = [
+        remote(w_ref, own, send.at[n], recv.at[n], peer) for n, peer in enumerate(along_z)
+    ]
+    for copy in copies:
+        copy.start()
+    keep.wait()
+    for copy in copies:
+        copy.wait()
+
+
 def gather_kernel(low_column, width, with_levels, *refs):
     if with_levels:
-        (w_ref, one_ref, two_ref, out_ref, all_one, all_two, own_sem, send, recv,
+        (_, one_ref, two_ref, out_ref, all_one, all_two, send, recv,
          level_own, level_send, level_recv) = refs
     else:
-        w_ref, _, out_ref, own_sem, send, recv = refs
+        _, out_ref, send, recv = refs
     sa, sb = lax.axis_index("sa"), lax.axis_index("sb")
     z_lo, x, core = sa // 8, (sa // 2) % 4, sa % 2
     z_hi, y = sb // 4, sb % 4
@@ -78,12 +101,11 @@
     def at(z_at, x_at, y_at, core_at):
         return ((z_at % 4) * 8 + x_at * 2 + core_at, (z_at // 4) * 4 + y_at)
 
-    along_z = [at((z + d) % 8, x, y, core) for d in range(1, 8)]
     step_x = [at(z, (x + d) % 4, y, core) for d in (1, 3)]
     step_y = [at(z, x, (y + d) % 4, core) for d in (1, 3)]
     partner = at(z, x, y, 1 - core)
     along_sb = [(sa, (sb + d) % 8) for d in range(1, 8)]
-    greeted = along_z + step_x + step_y + [partner]
+    greeted = step_x + step_y + [partner]
     barrier = signal_all(greeted + (along_sb if with_levels else []))
     if with_levels:
         source_sb = sa // 4
@@ -118,11 +140,6 @@
         shared.append(push(piece, piece, partner))
 
     every = pl.ds(low_column, width)
-    own = out_ref.at[z_lo, x, core, z_hi, y, :, every]
-    keep = pltpu.make_async_copy(w_ref.at[:, every], own, own_sem)
-    keep.start()
-    first = [push(w_ref.at[:, every], own, peer) for peer in along_z]
-
     if with_levels:
         ones = []
         keep_one = pltpu.make_async_copy(one_ref, all_one.at[sb], level_own.at[0])
@@ -160,10 +177,6 @@
             return carry
 
         lax.fori_loop(0, 32, send_two, 0)
-
-    keep.wait()
-    for copy in first:
-        copy.wait_recv()
 
     half, quarter = width // 2, width // 4
 
@@ -243,50 +256,63 @@
         lax.fori_loop(0, 32, wait_two, 0)
 
 
-GATHER_COPIES = 7 + 16 + 13
-
-
-def gather_first(weight, level_one, level_two, width):
+GATHER_COPIES = 16 + 13
+
+
+def gather_z(weight):
     rows, columns = weight.shape
+    dma = pltpu.SemaphoreType.DMA
+    return pl.pallas_call(
+        gather_z_kernel,
+        out_shape=jax.ShapeDtypeStruct((4, 4, 2, 2, 4, rows, columns), weight.dtype),
+        in_specs=[pl.BlockSpec(memory_space=pltpu.VMEM)],
+        out_specs=pl.BlockSpec(memory_space=pl.ANY),
+        scratch_shapes=[dma(()), dma((7,)), dma((7,))],
+        compiler_params=pltpu.CompilerParams(collective_id=3, has_side_effects=True),
+        name="gather_z",
+    )(weight)
+
+
+GATHER_COST = pl.CostEstimate(flops=10**9, bytes_accessed=2**24, transcendentals=0)
+
+
+def gather_first(gathered, level_one, level_two, width):
     whole = pl.BlockSpec(memory_space=pltpu.VMEM)
+    anywhere = pl.BlockSpec(memory_space=pl.ANY)
     dma = pltpu.SemaphoreType.DMA
     return pl.pallas_call(
         functools.partial(gather_kernel, 0, width, True),
         out_shape=(
-            jax.ShapeDtypeStruct((4, 4, 2, 2, 4, rows, columns), weight.dtype),
+            jax.ShapeDtypeStruct(gathered.shape, gathered.dtype),
             jax.ShapeDtypeStruct((8, *level_one.shape), level_one.dtype),
             jax.ShapeDtypeStruct((32, level_two.shape[0], *level_two.shape[2:]), level_two.dtype),
         ),
-        in_specs=[whole] * 3,
-        out_specs=(pl.BlockSpec(memory_space=pl.ANY), whole, whole),
+        in_specs=[anywhere, whole, whole],
+        out_specs=(anywhere, whole, whole),
+        input_output_aliases={0: 0},
         scratch_shapes=[
-            dma(()), dma((GATHER_COPIES,)), dma((GATHER_COPIES,)),
-            dma((2,)), dma((39,)), dma((39,)),
+            dma((GATHER_COPIES,)), dma((GATHER_COPIES,)), dma((2,)), dma((39,)), dma((39,)),
         ],
         compiler_params=pltpu.CompilerParams(collective_id=0, has_side_effects=True),
-        cost_estimate=pl.CostEstimate(
-            flops=10**9, bytes_accessed=8 * rows * columns * 256, transcendentals=0
-        ),
+        cost_estimate=GATHER_COST,
         name="gather_first",
-    )(weight, level_one, level_two)
-
-
-def gather_rest(weight, gathered, low):
-    rows, columns = weight.shape
+    )(gathered, level_one, level_two)
+
+
+def gather_rest(gathered, low):
     dma = pltpu.SemaphoreType.DMA
+    anywhere = pl.BlockSpec(memory_space=pl.ANY)
     return pl.pallas_call(
-        functools.partial(gather_kernel, low, columns - low, False),
+        functools.partial(gather_kernel, low, gathered.shape[-1] - low, False),
         out_shape=jax.ShapeDtypeStruct(gathered.shape, gathered.dtype),
-        in_specs=[pl.BlockSpec(memory_space=pltpu.VMEM), pl.BlockSpec(memory_space=pl.ANY)],
-        out_specs=pl.BlockSpec(memory_space=pl.ANY),
-        input_output_aliases={1: 0},
-        scratch_shapes=[dma(()), dma((GATHER_COPIES,)), dma((GATHER_COPIES,))],
+        in_specs=[anywhere],
+        out_specs=anywhere,
+        input_output_aliases={0: 0},
+        scratch_shapes=[dma((GATHER_COPIES,)), dma((GATHER_COPIES,))],
         compiler_params=pltpu.CompilerParams(collective_id=1, has_side_effects=True),
-        cost_estimate=pl.CostEstimate(
-            flops=10**9, bytes_accessed=8 * rows * columns * 256, transcendentals=0
-        ),
+        cost_estimate=GATHER_COST,
         name="gather_rest",
-    )(weight, gathered)
+    )(gathered)
 
 
 def reduce_kernel(scale, one_ref, two_ref, sum_one, sum_two, got_one, got_two, send, recv):
@@ -413,10 +439,10 @@
     inverse_rms = lax.rsqrt(jnp.mean(tokens_float * tokens_float, axis=3, keepdims=True) + EPSILON)
     normed = (tokens_float * inverse_rms * norm_gain).astype(jnp.bfloat16)
 
-    parts, weight_late = after((pack_blocks(normed), gate_weight))
+    parts, gathered = after((pack_blocks(normed), gather_z(gate_weight)))
     normed_block = exchange(parts)
     gathered, block_one, block_two = gather_first(
-        weight_late,
+        gathered,
         level_one.reshape(own_j, -1, 128),
         level_two.reshape(own_i, level_two.shape[1], -1, 128),
         channels // 2,
@@ -427,9 +453,9 @@
     normed_block = unpack_blocks(normed_block, own_i, own_j)
     first_mix = dot("joi,ijc->ojc", block_one, normed_block).astype(jnp.bfloat16)
     second_mix = dot("ioj,ijc->ioc", block_two, first_mix).astype(jnp.bfloat16)
-    parts, weight_late, gathered = after((pack_tokens(second_mix), gate_weight, gathered))
+    parts, gathered = after((pack_tokens(second_mix), gathered))
     second_mix = exchange(parts)
-    gathered = gather_rest(weight_late, gathered, channels // 2).reshape(-1, channels)
+    gathered = gather_rest(gathered, channels // 2).reshape(-1, channels)
     gate_pre = dot("tr,rc->tc", normed.reshape(-1, channels), gathered).reshape(tokens.shape)
     gate_pre, second_mix = after((gate_pre, second_mix))
     second_mix = unpack_tokens(second_mix, own_i, own_j)

time: 300 us -> 273 us (0.910)
  Pallas kernels: 146 us -> 123 us
  local copies, waits for them, and re-layouts: 47.1 us -> 44 us
    pallas_call x1, Pallas kernels: 60.5 us -> 45.1 us  [gather_first(): pl.pallas_call(functools.partial(gather_kernel, 0, width, True), out_shap...]
    pallas_call x1 -> x2, Pallas kernels: 53.8 us -> 46.3 us  [the longest x1 31.9 us: gather_rest(): pl.pallas_call(functools.partial(gather_kernel, low, gathered.shape[-1] -...]
  transfers between devices with their start and end apart: 4 -> 4, of which waited for: 1 -> 1; matrix products, arithmetic and copies ran while one was open for 10% -> 11% of each run, Pallas kernels for 49% -> 40%
where the time goes in v1:
time: 273 us; the launch traced here: 272 us
  Pallas kernels  123 us (45%)
  starting transfers between devices  44.1 us (16%)
  local copies, waits for them, and re-layouts  44 us (16%)
  matrix products  33.3 us (12%)
  waiting for transfers between devices  19.9 us (7%)
  other arithmetic  6.99 us (3%)
    pallas_call x1, Pallas kernels, gather_first(): pl.pallas_call(functools.partial(gather_kernel, 0, width, True), out_shap...  45.1 us
    all_to_all x4, starting transfers between devices, exchange(): return lax.all_to_all(parts, ALL, split_axis=0, concat_axis=0, tiled=True)  44.1 us
    dot_general x11, matrix products, dot(): return jnp.einsum(pattern, left, right, preferred_element_type=jnp.float32)  33.3 us
    pallas_call x1, Pallas kernels, gather_rest(): pl.pallas_call(functools.partial(gather_kernel, low, gathered.shape[-1] -...  31.9 us
    pallas_call x1, Pallas kernels, reduce_parts(): pl.pallas_call(functools.partial(reduce_kernel, scale), out_shape=(jax.Sh...  31.4 us
    all_to_all x4, waiting for transfers between devices, exchange(): return lax.all_to_all(parts, ALL, split_axis=0, concat_axis=0, tiled=True)  19.9 us
    pallas_call x1, Pallas kernels, gather_z(): pl.pallas_call(gather_z_kernel, out_shape=jax.ShapeDtypeStruct((4, 4, 2,...  14.4 us
    reshape x4, local copies, waits for them, and re-layouts, pack_tokens(): parts = values.reshape(sa, i, sb, j, c).transpose(0, 2, 1, 3, 4)  5.54 us
  transfers between devices with their start and end apart: 4, of which 1 were waited for; matrix products, arithmetic and copies ran while one was open for 11% of the time, Pallas kernels for 40%

profile of v1, /device:TPU:9, one launch (start us, length us, event | category | flops | bytes accessed | tf_op | source)
XLA Modules:
  0.0 272.0 jit_solution(4110939257065870676)
XLA Ops:
  6.6 14.4 %gather_z.1.refs_0_ = bf16[4,4,2,2,4,8,2048]{6,5,4,3,2,1,0:T(8,128)(2,1)} custom-call(bf16[8,2048]{1,0:T(8,128)(2,1)} %w_ref.1), custom_call_target="tpu_custom_call" | custom-call | tf_op jit(solution)/shard_map/gather_z/pallas_call | solution.py:265
  21.0 12.9 %all-to-all-start = ((bf16[256,8,256]{2,1,0:T(8,128)(2,1)}), bf16[256,8,256]{2,1,0:T(8,128)(2,1)S(1)}, u32[]{:S(2)}, u32[]{:S(2)}) async-start(bf16[256,8,256]{2,1,0:T(8,128)(2,1)} %copy.73), calls=%async_computation | async-start | bytes 2097152 | tf_op jit(solution)/shard_map/all_to_all | solution.py:46
  35.3 45.1 %gather_first.1 = (bf16[4,4,2,2,4,8,2048]{6,5,4,3,2,1,0:T(8,128)(2,1)}, bf16[8,4,32,128]{3,2,1,0:T(8,128)(2,1)}, bf16[32,2,8,128]{3,2,1,0:T(8,128)(2,1)}) custom-call(bf16[4,4,2,2,4,8,2048]{6,5,4,3,2,1,0:T(8,128)(2,1)} %gather_z.1.refs_0_, bf16[4,32,128]{2,1,0:T(8,128)(2,1)} %reshape.116.refs_1_, ...), custom_call_target="tpu_custom_call", output_to_operand_aliasing={{0}: (0, {})} | custom-call | flops 1000000000 | bytes 16777216 | tf_op jit(solution)/shard_map/gather_first/pallas_call | solution.py:283
  90.0 10.1 %all-to-all-start.1 = ((bf16[256,8,256]{2,1,0:T(8,128)(2,1)}), bf16[256,8,256]{2,1,0:T(8,128)(2,1)}, u32[]{:S(2)}, u32[]{:S(2)}) async-start(bf16[256,8,256]{2,1,0:T(8,128)(2,1)} %copy.53), calls=%async_computation.1 | async-start | bytes 2097152 | tf_op jit(solution)/shard_map/all_to_all | solution.py:46
  100.1 31.9 %gather_rest.1 = bf16[4,4,2,2,4,8,2048]{6,5,4,3,2,1,0:T(8,128)(2,1)} custom-call(bf16[4,4,2,2,4,8,2048]{6,5,4,3,2,1,0:T(8,128)(2,1)} %get-tuple-element.33.refs_0_), custom_call_target="tpu_custom_call", output_to_operand_aliasing={{}: (0, {})} | custom-call | flops 1000000000 | bytes 16777216 | tf_op jit(solution)/shard_map/gather_rest/pallas_call | solution.py:305
  132.1 7.2 %fusion.19 = f32[2,4,32,2048]{3,2,1,0:T(8,128)} fusion(bf16[2,4,32,2048]{3,2,1,0:T(8,128)(2,1)S(1)} %copy-done.8, bf16[2048,2048,1,1]{1,0,3,2:T(8,128)(2,1)} %bitcast.89), kind=kOutput, calls=%fused_computation.41 | convolution fusion | flops 2147483648 | bytes 11534336 | tf_op jit(solution)/shard_map/tr,rc->tc/dot_general | solution.py:428
  139.3 2.1 reshape.125
  141.4 2.5 copy.54
  143.9 2.3 reshape.126
  146.2 5.1 %fusion.3 = (bf16[2,4,32,2048]{3,2,1,0:T(8,128)(2,1)}, bf16[2,4,32,2048]{3,2,1,0:T(8,128)(2,1)}, bf16[2,4,32,2048]{3,2,1,0:T(8,128)(2,1)S(1)}) fusion(bf16[2,4,32,2048]{3,2,1,0:T(8,128)(2,1)} %param.13, f32[2,4,32,2048]{3,2,1,0:T(8,128)} %fusion.19, bf16[2,4,32,2048]{3,2,1,0:T(8,128)(2,1)S(1)} %copy-done.1, bf16[2,4,32,32]{3,2,1,0:T(8,128)(2,1)S(1)} %copy-done, ...), kind=kOutput, calls=%fused_computation.13 | convolution fusion | flops 42991616 | bytes 8404992 | tf_op jit(solution)/shard_map/ijok,ijkc->ijoc/dot_general | solution.py:428
  153.9 12.0 %all-to-all-start.2 = ((bf16[256,8,256]{2,1,0:T(8,128)(2,1)}), bf16[256,8,256]{2,1,0:T(8,128)(2,1)}, u32[]{:S(2)}, u32[]{:S(2)}) async-start(bf16[256,8,256]{2,1,0:T(8,128)(2,1)} %copy.74), calls=%async_computation.2 | async-start | bytes 2097152 | tf_op jit(solution)/shard_map/all_to_all | solution.py:46
  165.9 2.7 convolution_multiply_fusion
  168.6 7.1 %fusion.20 = f32[256,2048]{1,0:T(8,128)} fusion(bf16[256,2048]{1,0:T(8,128)(2,1)S(1)} %bitcast.104, bf16[2048,2048]{1,0:T(8,128)(2,1)} %bitcast.90), kind=kOutput, calls=%fused_computation.42 | convolution fusion | flops 2147483648 | bytes 11534336 | tf_op jit(solution)/shard_map/tc,rc->tr/dot_general | solution.py:428
  175.8 19.9 %all-to-all-done.2 = bf16[256,8,256]{2,1,0:T(8,128)(2,1)} async-done(((bf16[256,8,256]{2,1,0:T(8,128)(2,1)}), bf16[256,8,256]{2,1,0:T(8,128)(2,1)}, u32[]{:S(2)}, u32[]{:S(2)}) %all-to-all-start.2) | async-done | bytes 1048608 | tf_op jit(solution)/shard_map/all_to_all | solution.py:46
  197.1 2.3 copy.58
  199.4 2.1 reshape.131
  206.3 2.2 reshape.132
  211.9 9.1 %all-to-all-start.3 = ((bf16[256,8,256]{2,1,0:T(8,128)(2,1)}), bf16[256,8,256]{2,1,0:T(8,128)(2,1)}, u32[]{:S(2)}, u32[]{:S(2)}) async-start(bf16[256,8,256]{2,1,0:T(8,128)(2,1)} %copy.63), calls=%async_computation.3 | async-start | bytes 2097152 | tf_op jit(solution)/shard_map/all_to_all | solution.py:46
  221.0 2.8 %convolution_convert_fusion.5 = bf16[64,32,32]{2,1,0:T(8,128)(2,1)} fusion(bf16[64,32,256]{2,1,0:T(8,128)(2,1)} %reshape.131, bf16[64,32,256]{2,0,1:T(8,128)(2,1)S(1)} %fusion.14), kind=kOutput, calls=%fused_computation.31 | convolution fusion | flops 33619968 | bytes 2228224 | tf_op jit(solution)/shard_map/ioc,ijc->ioj/dot_general | solution.py:428
  223.8 2.0 reshape.135.two_ref
  225.9 1.9 convolution_convert_fusion.6
  228.8 31.4 %reduce_parts.1 = (f32[128,128]{1,0:T(8,128)}, f32[4,2,8,128]{3,2,1,0:T(8,128)}) custom-call(bf16[8,128,128]{2,1,0:T(8,128)(2,1)} %reshape.134.one_ref, bf16[32,2,8,128]{3,2,1,0:T(8,128)(2,1)} %reshape.135.two_ref), custom_call_target="tpu_custom_call" | custom-call | flops 100000000 | bytes 1048576 | tf_op jit(solution)/shard_map/reduce_parts/pallas_call | solution.py:407
  263.3 2.8 %copy.75 = f32[256,8,256]{2,0,1:T(8,128)} copy(bf16[256,8,256]{2,1,0:T(8,128)(2,1)} %all-to-all-done.3) | data formatting | bytes 3145728 | tf_op jit(solution)/shard_map/convert_element_type | solution.py:495
  267.8 2.2 fusion.11
  (65 shorter events, 36.8 us)
Async XLA Ops:
  0.6 145.6 %copy-start = (bf16[2,4,32,32]{3,2,1,0:T(8,128)(2,1)S(1)}, bf16[2,4,32,32]{3,2,1,0:T(8,128)(2,1)}, u32[]{:S(2)}) copy-start(bf16[2,4,32,32]{3,2,1,0:T(8,128)(2,1)} %param.12) | copy-start | bytes 49156
  3.7 1.0 copy-start.7
  21.0 12.9 %copy-start.12 = (bf16[2,4,32,32]{3,2,1,0:T(8,128)(2,1)S(1)}, bf16[2,4,32,32]{3,2,1,0:T(8,128)(2,1)}, u32[]{:S(2)}) copy-start(bf16[2,4,32,32]{3,2,1,0:T(8,128)(2,1)} %param.11) | copy-start | bytes 49156
  21.0 13.6 %copy-start.13 = (bf16[4,1,64,64]{3,2,1,0:T(8,128)(2,1)S(1)}, bf16[4,1,64,64]{3,2,1,0:T(8,128)(2,1)}, u32[]{:S(2)}) copy-start(bf16[4,1,64,64]{3,2,1,0:T(8,128)(2,1)} %param.10) | copy-start | bytes 98308
  21.0 62.0 %all-to-all-start = ((bf16[256,8,256]{2,1,0:T(8,128)(2,1)}), bf16[256,8,256]{2,1,0:T(8,128)(2,1)S(1)}, u32[]{:S(2)}, u32[]{:S(2)}) async-start(bf16[256,8,256]{2,1,0:T(8,128)(2,1)} %copy.73), calls=%async_computation | async-start | bytes 2097152 | tf_op jit(solution)/shard_map/all_to_all | solution.py:46
  81.6 3.6 %copy-start.4 = (bf16[64,32,32]{2,1,0:T(8,128)(2,1)}, bf16[64,32,32]{2,1,0:T(8,128)(2,1)S(1)}, u32[]{:S(2)}) copy-start(bf16[64,32,32]{2,1,0:T(8,128)(2,1)S(1)} %reshape.118) | copy-start | bytes 393220
  83.0 1.8 copy-start.5
  90.0 49.3 %all-to-all-start.1 = ((bf16[256,8,256]{2,1,0:T(8,128)(2,1)}), bf16[256,8,256]{2,1,0:T(8,128)(2,1)}, u32[]{:S(2)}, u32[]{:S(2)}) async-start(bf16[256,8,256]{2,1,0:T(8,128)(2,1)} %copy.53), calls=%async_computation.1 | async-start | bytes 2097152 | tf_op jit(solution)/shard_map/all_to_all | solution.py:46
  100.1 31.9 %copy-start.8 = (bf16[2,4,32,2048]{3,2,1,0:T(8,128)(2,1)S(1)}, bf16[2,4,32,2048]{3,2,1,0:T(8,128)(2,1)}, u32[]{:S(2)}) copy-start(bf16[2,4,32,2048]{3,2,1,0:T(8,128)(2,1)} %copy-done.7) | copy-start | bytes 3145732
  141.4 4.8 %copy-start.1 = (bf16[2,4,32,2048]{3,2,1,0:T(8,128)(2,1)S(1)}, bf16[2,4,32,2048]{3,2,1,0:T(8,128)(2,1)}, u32[]{:S(2)}) copy-start(bf16[2,4,32,2048]{3,2,1,0:T(8,128)(2,1)} %param.7) | copy-start | bytes 3145732
  151.3 1.0 copy-start.9
  153.9 41.7 %all-to-all-start.2 = ((bf16[256,8,256]{2,1,0:T(8,128)(2,1)}), bf16[256,8,256]{2,1,0:T(8,128)(2,1)}, u32[]{:S(2)}, u32[]{:S(2)}) async-start(bf16[256,8,256]{2,1,0:T(8,128)(2,1)} %copy.74), calls=%async_computation.2 | async-start | bytes 2097152 | tf_op jit(solution)/shard_map/all_to_all | solution.py:46
  165.9 2.7 copy-start.14
  201.5 2.9 %copy-start.6 = (bf16[32,64,64]{2,1,0:T(8,128)(2,1)S(1)}, bf16[32,64,64]{2,1,0:T(8,128)(2,1)}, u32[]{:S(2)}) copy-start(bf16[32,64,64]{2,1,0:T(8,128)(2,1)} %copy-done.5) | copy-start | bytes 786436
  203.5 1.0 copy-start.2
  211.9 48.2 %all-to-all-start.3 = ((bf16[256,8,256]{2,1,0:T(8,128)(2,1)}), bf16[256,8,256]{2,1,0:T(8,128)(2,1)}, u32[]{:S(2)}, u32[]{:S(2)}) async-start(bf16[256,8,256]{2,1,0:T(8,128)(2,1)} %copy.63), calls=%async_computation.3 | async-start | bytes 2097152 | tf_op jit(solution)/shard_map/all_to_all | solution.py:46
  266.1 1.7 copy-start.11
  267.8 2.2 copy-start.3
  267.8 2.5 copy-start.10

commit v2 on v1

--- a/solution.py
+++ b/solution.py
@@ -19,20 +19,6 @@
     sa, sb = lax.axis_size("sa"), lax.axis_size("sb")
     parts = values.reshape(i, j, sa, sb, c // sb).transpose(2, 3, 0, 1, 4)
     return parts.reshape(sa * sb, i * j, c // sb)
-
-
-def unpack_blocks(parts, i, j):
-    sa, sb = lax.axis_size("sa"), lax.axis_size("sb")
-    c = parts.shape[2]
-    parts = parts.reshape(sa, sb, i, j, c).transpose(0, 2, 1, 3, 4)
-    return parts.reshape(sa * i, sb * j, c)
-
-
-def pack_tokens(values):
-    sa, sb = lax.axis_size("sa"), lax.axis_size("sb")
-    i, j, c = values.shape[0] // sa, values.shape[1] // sb, values.shape[2]
-    parts = values.reshape(sa, i, sb, j, c).transpose(0, 2, 1, 3, 4)
-    return parts.reshape(sa * sb, i * j, c)
 
 
 def unpack_tokens(parts, i, j):
@@ -424,6 +410,108 @@
     )(part_one, part_two)
 
 
+def iota_pair(rows, columns):
+    shape = (rows, columns)
+    return (
+        lax.broadcasted_iota(jnp.int32, shape, 0),
+        lax.broadcasted_iota(jnp.int32, shape, 1),
+    )
+
+
+def one_hot(test):
+    return jnp.where(test, 1.0, 0.0).astype(jnp.bfloat16)
+
+
+def spread_one():
+    r, q = iota_pair(256, 256)
+    turn = one_hot(((r & 3) == (q >> 6)) & ((r >> 2) == (q & 63)))
+    i, c = iota_pair(64, 256)
+    widen = one_hot((c >> 2) == i)
+    return turn, widen, (q & 3) == (r >> 6)
+
+
+def spread_two():
+    r, q = iota_pair(256, 256)
+    turn = one_hot(
+        ((r >> 6) == (q >> 6))
+        & (((r >> 3) & 7) == ((q >> 2) & 7))
+        & (((r >> 2) & 1) == ((q >> 5) & 1))
+        & ((r & 3) == (q & 3))
+    )
+    j, c = iota_pair(32, 256)
+    widen = one_hot((((c >> 3) & 7) == (j >> 2)) & ((c & 3) == (j & 3)))
+    return turn, widen, ((r >> 6) == (q >> 6)) & (((r >> 5) & 1) == ((q >> 2) & 1))
+
+
+def product(left, right, contract=(1, 0)):
+    return lax.dot_general(
+        left,
+        right,
+        (((contract[0],), (contract[1],)), ((), ())),
+        preferred_element_type=jnp.float32,
+    )
+
+
+def widen_kernel(one_ref, two_ref, wide_one, wide_two):
+    for blocks, wide, (turn, widen, keep) in (
+        (one_ref, wide_one, spread_one()),
+        (two_ref, wide_two, spread_two()),
+    ):
+        for n in range(8):
+            spread = jnp.where(keep, product(blocks[n], widen), 0.0).astype(jnp.bfloat16)
+            wide[n] = product(turn, spread).astype(jnp.bfloat16)
+
+
+def rows_of(value):
+    return value.astype(jnp.float32).reshape(256, 256).astype(jnp.bfloat16)
+
+
+def forward_kernel(got, wide_one, wide_two, first, out):
+    for b in range(8):
+        mixed = product(wide_one[b], rows_of(got[:, b]))
+        first[:, b] = mixed.reshape(32, 8, 256).astype(jnp.bfloat16)
+    for g in range(8):
+        mixed = product(wide_two[g], rows_of(first[4 * g : 4 * g + 4]))
+        out[4 * g : 4 * g + 4] = mixed.reshape(4, 8, 8, 256).astype(jnp.bfloat16)
+
+
+def backward_kernel(got, wide_one, wide_two, first, out):
+    for g in range(8):
+        mixed = product(wide_two[g], rows_of(got[4 * g : 4 * g + 4]), (0, 0))
+        first[4 * g : 4 * g + 4] = mixed.reshape(4, 8, 8, 256).astype(jnp.bfloat16)
+    for b in range(8):
+        mixed = product(wide_one[b], rows_of(first[:, b]), (0, 0))
+        out[:, b] = mixed.reshape(32, 8, 256).astype(jnp.bfloat16)
+
+
+def parts_kernel(grad_second, first_mix, grad_first, normed, part_one, part_two):
+    turn, widen, keep = spread_two()
+    for g in range(8):
+        rows = slice(4 * g, 4 * g + 4)
+        outer = product(rows_of(grad_second[rows]), rows_of(first_mix[rows]), (1, 1))
+        outer = product(turn, outer.astype(jnp.bfloat16), (0, 0))
+        outer = jnp.where(keep, outer, 0.0).astype(jnp.bfloat16)
+        part_two[g] = product(outer, widen, (1, 1)).astype(jnp.bfloat16)
+    turn, widen, keep = spread_one()
+    for b in range(8):
+        outer = product(rows_of(grad_first[:, b]), rows_of(normed[:, b]), (1, 1))
+        outer = product(turn, outer.astype(jnp.bfloat16), (0, 0))
+        outer = jnp.where(keep, outer, 0.0).astype(jnp.bfloat16)
+        part_one[b] = product(outer, widen, (1, 1)).astype(jnp.bfloat16)
+
+
+def local_call(kernel, out_shapes, *operands):
+    whole = pl.BlockSpec(memory_space=pltpu.VMEM)
+    return pl.pallas_call(
+        kernel,
+        out_shape=tuple(jax.ShapeDtypeStruct(shape, jnp.bfloat16) for shape in out_shapes),
+        in_specs=[whole] * len(operands),
+        out_specs=(whole,) * len(out_shapes),
+        cost_estimate=pl.CostEstimate(flops=10**9, bytes_accessed=2**22, transcendentals=0),
+        name=kernel.__name__,
+    )(*operands)
+
+
 def dot(pattern, left, right):
     return jnp.einsum(pattern, left, right, preferred_element_type=jnp.float32)
 
@@ -447,13 +535,17 @@
         level_two.reshape(own_i, level_two.shape[1], -1, 128),
         channels // 2,
     )
-    block_one = block_one.reshape(sb * own_j, m1, m1)
-    block_two = block_two.reshape(sa * own_i, m2, m2)
-
-    normed_block = unpack_blocks(normed_block, own_i, own_j)
-    first_mix = dot("joi,ijc->ojc", block_one, normed_block).astype(jnp.bfloat16)
-    second_mix = dot("ioj,ijc->ioc", block_two, first_mix).astype(jnp.bfloat16)
-    parts, gathered = after((pack_tokens(second_mix), gathered))
+    block_one = block_one.reshape(sb, own_j * m1, m1)
+    block_two = block_two.reshape(8, -1, m2)
+    wide = (8, 256, 256)
+    wide_one, wide_two = local_call(widen_kernel, (wide, wide), block_one, block_two)
+
+    grid = (sa, sb, *normed_block.shape[1:])
+    normed_block = normed_block.reshape(grid)
+    first_mix, second_mix = local_call(
+        forward_kernel, (grid, grid), normed_block, wide_one, wide_two
+    )
+    parts, gathered = after((second_mix.reshape(parts.shape), gathered))
     second_mix = exchange(parts)
     gathered = gather_rest(gathered, channels // 2).reshape(-1, channels)
     gate_pre = dot("tr,rc->tc", normed.reshape(-1, channels), gathered).reshape(tokens.shape)
@@ -477,13 +569,22 @@
     grad_three = dot("ijoc,ijkc->ijok", grad_mixed, second_mix) * grad_scale
     grad_block, back_term, grad_three = after((grad_block, back_term, grad_three))
 
-    grad_block = unpack_blocks(grad_block, own_i, own_j)
-    grad_first = dot("ioj,ioc->ijc", block_two, grad_block).astype(jnp.bfloat16)
-    grad_normed = dot("joi,ojc->ijc", block_one, grad_first).astype(jnp.bfloat16)
-    parts, grad_block, grad_first = after((pack_tokens(grad_normed), grad_block, grad_first))
+    grad_block = grad_block.reshape(grid)
+    grad_first, grad_normed = local_call(
+        backward_kernel, (grid, grid), grad_block, wide_one, wide_two
+    )
+    parts, grad_block, grad_first = after(
+        (grad_normed.reshape(parts.shape), grad_block, grad_first)
+    )
     grad_normed = exchange(parts)
-    part_two = dot("ioc,ijc->ioj", grad_block, first_mix).astype(jnp.bfloat16)
-    part_one = dot("ojc,ijc->joi", grad_first, normed_block).astype(jnp.bfloat16)
+    part_one, part_two = local_call(
+        parts_kernel,
+        (block_one.shape, block_two.shape),
+        grad_block,
+        first_mix,
+        grad_first,
+        normed_block,
+    )
     grad_one, grad_two = reduce_parts(
         part_one.reshape(sb, -1, 128), part_two.reshape(sa, own_i, -1, 128), grad_scale
     )

time: 273 us -> 254 us (0.930)
  local copies, waits for them, and re-layouts: 44 us -> 22.2 us
  Pallas kernels: 123 us -> 140 us
  matrix products: 33.3 us -> 20.6 us
    pallas_call x0 -> x4, Pallas kernels: none -> 18.5 us  [local_call(): pl.pallas_call(kernel, out_shape=tuple((jax.ShapeDtypeStruct(shape, jnp.b...]
    dot_general x11 -> x5, matrix products: 33.3 us -> 20.6 us  [dot(): return jnp.einsum(pattern, left, right, preferred_element_type=jnp.float32)]
    reshape x8 -> x2, local copies, waits for them, and re-layouts: 10.6 us -> 4.01 us  [the longest x1 2.01 us: body(): block_two = block_two.reshape(8, -1, m2)]
    transpose x3 -> x0, local copies, waits for them, and re-layouts: 5.89 us -> none  [the longest x2 3.4 us: unpack_blocks(): parts = parts.reshape(sa, sb, i, j, c).transpose(0, 2, 1, 3, 4)]
    optimization_barrier x3 -> x0, local copies, waits for them, and re-layouts: 4.54 us -> none  [the longest x1 1.55 us: body(): parts, gathered = after((pack_tokens(second_mix), gathered))]
  transfers between devices with their start and end apart: 4 -> 4, of which waited for: 1 -> 1; matrix products, arithmetic and copies ran while one was open for 11% -> 10% of each run, Pallas kernels for 40% -> 47%
where the time goes in v2:
time: 254 us; the launch traced here: 253 us
  Pallas kernels  140 us (55%)
  starting transfers between devices  41.6 us (16%)
  local copies, waits for them, and re-layouts  22.2 us (9%)
  waiting for transfers between devices  21.3 us (8%)
  matrix products  20.6 us (8%)
  other arithmetic  6.99 us (3%)
    pallas_call x1, Pallas kernels, gather_first(): pl.pallas_call(functools.partial(gather_kernel, 0, width, True), out_shap...  45.2 us
    all_to_all x4, starting transfers between devices, exchange(): return lax.all_to_all(parts, ALL, split_axis=0, concat_axis=0, tiled=True)  41.6 us
    pallas_call x1, Pallas kernels, gather_rest(): pl.pallas_call(functools.partial(gather_kernel, low, gathered.shape[-1] -...  32.8 us
    pallas_call x1, Pallas kernels, reduce_parts(): pl.pallas_call(functools.partial(reduce_kernel, scale), out_shape=(jax.Sh...  28.7 us
    all_to_all x4, waiting for transfers between devices, exchange(): return lax.all_to_all(parts, ALL, split_axis=0, concat_axis=0, tiled=True)  21.3 us
    dot_general x5, matrix products, dot(): return jnp.einsum(pattern, left, right, preferred_element_type=jnp.float32)  20.6 us
    pallas_call x4, Pallas kernels, local_call(): pl.pallas_call(kernel, out_shape=tuple((jax.ShapeDtypeStruct(shape, jnp.b...  18.5 us
    pallas_call x1, Pallas kernels, gather_z(): pl.pallas_call(gather_z_kernel, out_shape=jax.ShapeDtypeStruct((4, 4, 2,...  14.4 us
  transfers between devices with their start and end apart: 4, of which 1 were waited for; matrix products, arithmetic and copies ran while one was open for 10% of the time, Pallas kernels for 47%

profile of v2, /device:TPU:9, one launch (start us, length us, event | category | flops | bytes accessed | tf_op | source)
XLA Modules:
  0.0 253.1 jit_solution(7829159163436053476)
XLA Ops:
  5.6 14.4 %gather_z.1.refs_0_ = bf16[4,4,2,2,4,8,2048]{6,5,4,3,2,1,0:T(8,128)(2,1)} custom-call(bf16[8,2048]{1,0:T(8,128)(2,1)} %w_ref.1), custom_call_target="tpu_custom_call" | custom-call | tf_op jit(solution)/shard_map/gather_z/pallas_call | solution.py:251
  20.0 12.9 %all-to-all-start = ((bf16[256,8,256]{2,1,0:T(8,128)(2,1)}), bf16[256,8,256]{2,1,0:T(8,128)(2,1)S(1)}, u32[]{:S(2)}, u32[]{:S(2)}) async-start(bf16[256,8,256]{2,1,0:T(8,128)(2,1)} %copy.30), calls=%async_computation | async-start | bytes 2097152 | tf_op jit(solution)/shard_map/all_to_all | solution.py:32
  34.3 45.2 %gather_first.1 = (bf16[4,4,2,2,4,8,2048]{6,5,4,3,2,1,0:T(8,128)(2,1)}, bf16[8,4,32,128]{3,2,1,0:T(8,128)(2,1)}, bf16[32,2,8,128]{3,2,1,0:T(8,128)(2,1)}) custom-call(bf16[4,4,2,2,4,8,2048]{6,5,4,3,2,1,0:T(8,128)(2,1)} %gather_z.1.refs_0_, bf16[4,32,128]{2,1,0:T(8,128)(2,1)} %reshape.105.refs_1_, ...), custom_call_target="tpu_custom_call", output_to_operand_aliasing={{0}: (0, {})} | custom-call | flops 1000000000 | bytes 16777216 | tf_op jit(solution)/shard_map/gather_first/pallas_call | solution.py:269
  79.5 2.0 reshape.107.one_ref
  81.5 2.0 reshape.108.two_ref
  83.5 3.8 %widen_kernel.1 = (bf16[8,256,256]{2,1,0:T(8,128)(2,1)}, bf16[8,256,256]{2,1,0:T(8,128)(2,1)}) custom-call(bf16[8,256,64]{2,1,0:T(8,128)(2,1)} %reshape.107.one_ref, bf16[8,256,32]{2,1,0:T(8,128)(2,1)} %reshape.108.two_ref), custom_call_target="tpu_custom_call" | custom-call | flops 1000000000 | bytes 4194304 | tf_op jit(solution)/shard_map/widen_kernel/pallas_call | solution.py:505
  88.3 3.6 %forward_kernel.1 = (bf16[32,8,8,256]{3,2,1,0:T(8,128)(2,1)}, bf16[32,8,8,256]{3,2,1,0:T(8,128)(2,1)}) custom-call(bf16[32,8,8,256]{3,2,1,0:T(8,128)(2,1)} %bitcast.76, bf16[8,256,256]{2,1,0:T(8,128)(2,1)} %get-tuple-element.40.wide_one, bf16[8,256,256]{2,1,0:T(8,128)(2,1)} %get-tuple-element.41.wide_two), custom_call_target="tpu_custom_call" | custom-call | flops 1000000000 | bytes 4194304 | tf_op jit(solution)/shard_map/forward_kernel/pallas_call | solution.py:505
  91.9 9.1 %all-to-all-start.1 = ((bf16[256,8,256]{2,1,0:T(8,128)(2,1)}), bf16[256,8,256]{2,1,0:T(8,128)(2,1)S(1)}, u32[]{:S(2)}, u32[]{:S(2)}) async-start(bf16[256,8,256]{2,1,0:T(8,128)(2,1)} %bitcast.79), calls=%async_computation.1 | async-start | bytes 2097152 | tf_op jit(solution)/shard_map/all_to_all | solution.py:32
  101.1 32.8 %gather_rest.1 = bf16[4,4,2,2,4,8,2048]{6,5,4,3,2,1,0:T(8,128)(2,1)} custom-call(bf16[4,4,2,2,4,8,2048]{6,5,4,3,2,1,0:T(8,128)(2,1)} %get-tuple-element.44.refs_0_), custom_call_target="tpu_custom_call", output_to_operand_aliasing={{}: (0, {})} | custom-call | flops 1000000000 | bytes 16777216 | tf_op jit(solution)/shard_map/gather_rest/pallas_call | solution.py:291
  133.9 7.0 %fusion.13 = f32[2,4,32,2048]{3,2,1,0:T(8,128)} fusion(bf16[2,4,32,2048]{3,2,1,0:T(8,128)(2,1)S(1)} %fusion.8, bf16[2048,2048,1,1]{1,0,3,2:T(8,128)(2,1)} %bitcast.67), kind=kOutput, calls=%fused_computation.29 | convolution fusion | flops 2147483648 | bytes 11534336 | tf_op jit(solution)/shard_map/tr,rc->tc/dot_general | solution.py:516
  142.2 4.9 %fusion.3 = (bf16[2,4,32,2048]{3,2,1,0:T(8,128)(2,1)}, bf16[2,4,32,2048]{3,2,1,0:T(8,128)(2,1)}, bf16[2,4,32,2048]{3,2,1,0:T(8,128)(2,1)S(1)}) fusion(bf16[2,4,32,2048]{3,2,1,0:T(8,128)(2,1)} %param.13, f32[2,4,32,2048]{3,2,1,0:T(8,128)} %fusion.13, bf16[2,4,32,2048]{3,2,1,0:T(8,128)(2,1)S(1)} %copy-done.1, bf16[2,4,32,32]{3,2,1,0:T(8,128)(2,1)S(1)} %copy-done, ...), kind=kOutput, calls=%fused_computation.13 | convolution fusion | flops 42991616 | bytes 8404992 | tf_op jit(solution)/shard_map/ijok,ijkc->ijoc/dot_general | solution.py:516
  149.4 12.1 %all-to-all-start.2 = ((bf16[256,8,256]{2,1,0:T(8,128)(2,1)}), bf16[256,8,256]{2,1,0:T(8,128)(2,1)}, u32[]{:S(2)}, u32[]{:S(2)}) async-start(bf16[256,8,256]{2,1,0:T(8,128)(2,1)} %copy.32), calls=%async_computation.2 | async-start | bytes 2097152 | tf_op jit(solution)/shard_map/all_to_all | solution.py:32
  162.7 7.1 %fusion.14 = f32[256,2048]{1,0:T(8,128)} fusion(bf16[256,2048]{1,0:T(8,128)(2,1)S(1)} %bitcast.82, bf16[2048,2048]{1,0:T(8,128)(2,1)} %bitcast.68), kind=kOutput, calls=%fused_computation.30 | convolution fusion | flops 2147483648 | bytes 11534336 | tf_op jit(solution)/shard_map/tc,rc->tr/dot_general | solution.py:516
  169.8 21.3 %all-to-all-done.2 = bf16[256,8,256]{2,1,0:T(8,128)(2,1)} async-done(((bf16[256,8,256]{2,1,0:T(8,128)(2,1)}), bf16[256,8,256]{2,1,0:T(8,128)(2,1)}, u32[]{:S(2)}, u32[]{:S(2)}) %all-to-all-start.2) | async-done | bytes 1048608 | tf_op jit(solution)/shard_map/all_to_all | solution.py:32
  191.2 3.7 %backward_kernel.1 = (bf16[32,8,8,256]{3,2,1,0:T(8,128)(2,1)}, bf16[32,8,8,256]{3,2,1,0:T(8,128)(2,1)}) custom-call(bf16[32,8,8,256]{3,2,1,0:T(8,128)(2,1)} %bitcast.14.got.grad_second, bf16[8,256,256]{2,1,0:T(8,128)(2,1)} %get-tuple-element.40.wide_one, bf16[8,256,256]{2,1,0:T(8,128)(2,1)} %get-tuple-element.41.wide_two), custom_call_target="tpu_custom_call" | custom-call | flops 1000000000 | bytes 4194304 | tf_op jit(solution)/shard_map/backward_kernel/pallas_call | solution.py:505
  194.9 7.5 %all-to-all-start.3 = ((bf16[256,8,256]{2,1,0:T(8,128)(2,1)}), bf16[256,8,256]{2,1,0:T(8,128)(2,1)S(1)}, u32[]{:S(2)}, u32[]{:S(2)}) async-start(bf16[256,8,256]{2,1,0:T(8,128)(2,1)} %bitcast.78), calls=%async_computation.3 | async-start | bytes 2097152 | tf_op jit(solution)/shard_map/all_to_all | solution.py:32
  202.4 7.4 %parts_kernel.1 = (bf16[8,256,64]{2,1,0:T(8,128)(2,1)}, bf16[8,256,32]{2,1,0:T(8,128)(2,1)}) custom-call(bf16[32,8,8,256]{3,2,1,0:T(8,128)(2,1)} %bitcast.14.got.grad_second, bf16[32,8,8,256]{3,2,1,0:T(8,128)(2,1)} %get-tuple-element.56.first_mix, bf16[32,8,8,256]{3,2,1,0:T(8,128)(2,1)} %get-tuple-element.57.grad_first, bf16[32,8,8,256]{3,2,1,0:T(8,128)(2,1)} %bitcast.77), custom_call_target="tpu_custom_call" | custom-call | flops 1000000000 | bytes 4194304 | tf_op jit(solution)/shard_map/parts_kernel/pallas_call | solution.py:505
  209.8 2.0 reshape.118.one_ref
  211.8 2.0 reshape.119.two_ref
  213.8 28.7 %reduce_parts.1 = (f32[128,128]{1,0:T(8,128)}, f32[4,2,8,128]{3,2,1,0:T(8,128)}) custom-call(bf16[8,128,128]{2,1,0:T(8,128)(2,1)} %reshape.118.one_ref, bf16[32,2,8,128]{3,2,1,0:T(8,128)(2,1)} %reshape.119.two_ref), custom_call_target="tpu_custom_call" | custom-call | flops 100000000 | bytes 1048576 | tf_op jit(solution)/shard_map/reduce_parts/pallas_call | solution.py:393
  242.5 1.6 reshape.121
  247.2 1.7 reshape.123
  248.9 2.2 fusion.11
  251.4 1.7 fusion.5
  (38 shorter events, 15.5 us)
Async XLA Ops:
  0.6 141.1 %copy-start = (bf16[2,4,32,32]{3,2,1,0:T(8,128)(2,1)S(1)}, bf16[2,4,32,32]{3,2,1,0:T(8,128)(2,1)}, u32[]{:S(2)}) copy-start(bf16[2,4,32,32]{3,2,1,0:T(8,128)(2,1)} %param.12) | copy-start | bytes 49156
  20.0 12.9 %copy-start.6 = (bf16[2,4,32,32]{3,2,1,0:T(8,128)(2,1)S(1)}, bf16[2,4,32,32]{3,2,1,0:T(8,128)(2,1)}, u32[]{:S(2)}) copy-start(bf16[2,4,32,32]{3,2,1,0:T(8,128)(2,1)} %param.11) | copy-start | bytes 49156
  20.0 13.6 %copy-start.7 = (bf16[4,1,64,64]{3,2,1,0:T(8,128)(2,1)S(1)}, bf16[4,1,64,64]{3,2,1,0:T(8,128)(2,1)}, u32[]{:S(2)}) copy-start(bf16[4,1,64,64]{3,2,1,0:T(8,128)(2,1)} %param.10) | copy-start | bytes 98308
  20.0 67.3 %all-to-all-start = ((bf16[256,8,256]{2,1,0:T(8,128)(2,1)}), bf16[256,8,256]{2,1,0:T(8,128)(2,1)S(1)}, u32[]{:S(2)}, u32[]{:S(2)}) async-start(bf16[256,8,256]{2,1,0:T(8,128)(2,1)} %copy.30), calls=%async_computation | async-start | bytes 2097152 | tf_op jit(solution)/shard_map/all_to_all | solution.py:32
  87.3 1.0 copy-start.3
  91.9 49.0 %all-to-all-start.1 = ((bf16[256,8,256]{2,1,0:T(8,128)(2,1)}), bf16[256,8,256]{2,1,0:T(8,128)(2,1)S(1)}, u32[]{:S(2)}, u32[]{:S(2)}) async-start(bf16[256,8,256]{2,1,0:T(8,128)(2,1)} %bitcast.79), calls=%async_computation.1 | async-start | bytes 2097152 | tf_op jit(solution)/shard_map/all_to_all | solution.py:32
  140.9 1.2 copy-start.1
  149.4 41.8 %all-to-all-start.2 = ((bf16[256,8,256]{2,1,0:T(8,128)(2,1)}), bf16[256,8,256]{2,1,0:T(8,128)(2,1)}, u32[]{:S(2)}, u32[]{:S(2)}) async-start(bf16[256,8,256]{2,1,0:T(8,128)(2,1)} %copy.32), calls=%async_computation.2 | async-start | bytes 2097152 | tf_op jit(solution)/shard_map/all_to_all | solution.py:32
  161.5 1.2 copy-start.8
  194.9 47.6 %all-to-all-start.3 = ((bf16[256,8,256]{2,1,0:T(8,128)(2,1)}), bf16[256,8,256]{2,1,0:T(8,128)(2,1)S(1)}, u32[]{:S(2)}, u32[]{:S(2)}) async-start(bf16[256,8,256]{2,1,0:T(8,128)(2,1)} %bitcast.78), calls=%async_computation.3 | async-start | bytes 2097152 | tf_op jit(solution)/shard_map/all_to_all | solution.py:32
  247.2 1.7 copy-start.5
  248.9 2.2 copy-start.2
  248.9 2.5 copy-start.4

commit v3 on v2

--- a/solution.py
+++ b/solution.py
@@ -50,7 +50,10 @@
     )
 
 
-def gather_z_kernel(w_ref, out_ref, own_sem, send, recv):
+def gather_z_kernel(
+    w_ref, one_ref, two_ref, tokens_ref, gain_ref, out_ref, all_one, all_two, normed_ref,
+    own_sem, send, recv, level_send, level_recv,
+):
     sa, sb = lax.axis_index("sa"), lax.axis_index("sb")
     z_lo, z_hi = sa // 8, sb // 4
     z = z_hi * 4 + z_lo
@@ -59,26 +62,115 @@
     for d in range(1, 8):
         to = (z + d) % 8
         along_z.append(((to % 4) * 8 + sa % 8, (to // 4) * 4 + sb % 4))
-    barrier = signal_all(along_z)
-    pl.semaphore_wait(barrier, len(along_z))
-    keep = pltpu.make_async_copy(w_ref, own, own_sem)
+    along_y = [(sa, z_hi * 4 + (sb % 4 + d) % 4) for d in range(1, 4)]
+    across = (sb + 4) % 8
+    barrier = signal_all(along_z + along_y)
+    source_sb = sa // 4
+
+    def greet(n, carry):
+        @pl.when(jnp.logical_or(n != sa, source_sb != sb))
+        def _():
+            pl.semaphore_signal(barrier, inc=1, device_id=(n, source_sb), device_id_type=MESH)
+
+        return carry
+
+    lax.fori_loop(0, 32, greet, 0)
+    pl.semaphore_wait(barrier, 7 + 3 + 31 + jnp.where(source_sb != sb, 1, 0))
+
+    keep = pltpu.make_async_copy(w_ref, own, own_sem.at[0])
     keep.start()
+    keep_one = pltpu.make_async_copy(one_ref, all_one.at[sb], own_sem.at[1])
+    keep_one.start()
+    over = remote(one_ref, all_one.at[sb], level_send.at[32], level_recv.at[32], (sa, across))
+    over.start()
     copies = [
         remote(w_ref, own, send.at[n], recv.at[n], peer) for n, peer in enumerate(along_z)
     ]
+    copies += [
+        remote(one_ref, all_one.at[sb], level_send.at[33 + n], level_recv.at[33 + n], peer)
+        for n, peer in enumerate(along_y)
+    ]
     for copy in copies:
         copy.start()
+
+    def two_copy(n):
+        return remote(
+            two_ref.at[:, n // 8],
+            all_two.at[sa],
+            level_send.at[n],
+            level_recv.at[sa],
+            (4 * sb + n // 8, n % 8),
+        )
+
+    def two_kept(n):
+        return pltpu.make_async_copy(two_ref.at[:, n // 8], all_two.at[sa], own_sem.at[2])
+
+    def is_self(n):
+        return jnp.logical_and(4 * sb + n // 8 == sa, n % 8 == sb)
+
+    def send_two(n, carry):
+        @pl.when(jnp.logical_not(is_self(n)))
+        def _():
+            two_copy(n).start()
+
+        @pl.when(is_self(n))
+        def _():
+            two_kept(n).start()
+
+        return carry
+
+    lax.fori_loop(0, 32, send_two, 0)
+
+    def normalise(n, carry):
+        values = tokens_ref[n // 4, n % 4].astype(jnp.float32)
+        square = jnp.mean(values * values, axis=1, keepdims=True)
+        values = values * lax.rsqrt(square + EPSILON) * gain_ref[...]
+        normed_ref[n // 4, n % 4] = values.astype(jnp.bfloat16)
+        return carry
+
+    lax.fori_loop(0, 4, normalise, 0)
+    over.wait()
+    for n, peer in enumerate(along_y):
+        copy = remote(
+            all_one.at[across],
+            all_one.at[across],
+            level_send.at[36 + n],
+            level_recv.at[36 + n],
+            peer,
+        )
+        copy.start()
+        copies.append(copy)
+    lax.fori_loop(4, 8, normalise, 0)
+
+    def wait_two(n, carry):
+        @pl.when(jnp.logical_not(is_self(n)))
+        def _():
+            two_copy(n).wait_send()
+
+        @pl.when(is_self(n))
+        def _():
+            two_kept(n).wait()
+
+        @pl.when(jnp.logical_or(n != sa, source_sb != sb))
+        def _():
+            remote(
+                two_ref.at[:, 0],
+                all_two.at[n],
+                level_send.at[n],
+                level_recv.at[n],
+                (n, source_sb),
+            ).wait_recv()
+
+        return carry
+
+    lax.fori_loop(0, 32, wait_two, 0)
     keep.wait()
+    keep_one.wait()
     for copy in copies:
         copy.wait()
 
 
-def gather_kernel(low_column, width, with_levels, *refs):
-    if with_levels:
-        (_, one_ref, two_ref, out_ref, all_one, all_two, send, recv,
-         level_own, level_send, level_recv) = refs
-    else:
-        _, out_ref, send, recv = refs
+def gather_kernel(low_column, width, _, out_ref, send, recv):
     sa, sb = lax.axis_index("sa"), lax.axis_index("sb")
     z_lo, x, core = sa // 8, (sa // 2) % 4, sa % 2
     z_hi, y = sb // 4, sb % 4
@@ -90,26 +182,8 @@
     step_x = [at(z, (x + d) % 4, y, core) for d in (1, 3)]
     step_y = [at(z, x, (y + d) % 4, core) for d in (1, 3)]
     partner = at(z, x, y, 1 - core)
-    along_sb = [(sa, (sb + d) % 8) for d in range(1, 8)]
     greeted = step_x + step_y + [partner]
-    barrier = signal_all(greeted + (along_sb if with_levels else []))
-    if with_levels:
-        source_sb = sa // 4
-
-        def greet(n, carry):
-            @pl.when(jnp.logical_or(n != sa, source_sb != sb))
-            def _():
-                pl.semaphore_signal(
-                    barrier, inc=1, device_id=(n, source_sb), device_id_type=MESH
-                )
-
-            return carry
-
-        lax.fori_loop(0, 32, greet, 0)
-        outside = jnp.where(source_sb != sb, 1, 0)
-        pl.semaphore_wait(barrier, len(greeted) + 7 + 31 + outside)
-    else:
-        pl.semaphore_wait(barrier, len(greeted))
+    pl.semaphore_wait(signal_all(greeted), len(greeted))
 
     started = []
 
@@ -126,44 +200,6 @@
         shared.append(push(piece, piece, partner))
 
     every = pl.ds(low_column, width)
-    if with_levels:
-        ones = []
-        keep_one = pltpu.make_async_copy(one_ref, all_one.at[sb], level_own.at[0])
-        keep_one.start()
-        for d, peer in enumerate(along_sb):
-            copy = remote(
-                one_ref, all_one.at[sb], level_send.at[32 + d], level_recv.at[32 + d], peer
-            )
-            copy.start()
-            ones.append(copy)
-
-        def two_copy(n):
-            return remote(
-                two_ref.at[:, n // 8],
-                all_two.at[sa],
-                level_send.at[n],
-                level_recv.at[sa],
-                (4 * sb + n // 8, n % 8),
-            )
-
-        def is_self(n):
-            return jnp.logical_and(4 * sb + n // 8 == sa, n % 8 == sb)
-
-        def send_two(n, carry):
-            @pl.when(jnp.logical_not(is_self(n)))
-            def _():
-                two_copy(n).start()
-
-            @pl.when(is_self(n))
-            def _():
-                pltpu.make_async_copy(
-                    two_ref.at[:, n // 8], all_two.at[sa], level_own.at[1]
-                ).start()
-
-            return carry
-
-        lax.fori_loop(0, 32, send_two, 0)
-
     half, quarter = width // 2, width // 4
 
     def piece_x(stage, at_x, low, size):
@@ -211,93 +247,43 @@
     for copy in started:
         copy.wait_send()
 
-    if with_levels:
-        keep_one.wait()
-        for copy in ones:
-            copy.wait()
-
-        def wait_two(n, carry):
-            @pl.when(jnp.logical_not(is_self(n)))
-            def _():
-                two_copy(n).wait_send()
-
-            @pl.when(is_self(n))
-            def _():
-                pltpu.make_async_copy(
-                    two_ref.at[:, n // 8], all_two.at[sa], level_own.at[1]
-                ).wait()
-
-            @pl.when(jnp.logical_or(n != sa, source_sb != sb))
-            def _():
-                remote(
-                    two_ref.at[:, 0],
-                    all_two.at[n],
-                    level_send.at[n],
-                    level_recv.at[n],
-                    (n, source_sb),
-                ).wait_recv()
-
-            return carry
-
-        lax.fori_loop(0, 32, wait_two, 0)
-
 
 GATHER_COPIES = 16 + 13
 
 
-def gather_z(weight):
+def gather_z(weight, level_one, level_two, tokens, gain):
     rows, columns = weight.shape
+    whole = pl.BlockSpec(memory_space=pltpu.VMEM)
     dma = pltpu.SemaphoreType.DMA
     return pl.pallas_call(
         gather_z_kernel,
-        out_shape=jax.ShapeDtypeStruct((4, 4, 2, 2, 4, rows, columns), weight.dtype),
-        in_specs=[pl.BlockSpec(memory_space=pltpu.VMEM)],
-        out_specs=pl.BlockSpec(memory_space=pl.ANY),
-        scratch_shapes=[dma(()), dma((7,)), dma((7,))],
+        out_shape=(
+            jax.ShapeDtypeStruct((4, 4, 2, 2, 4, rows, columns), weight.dtype),
+            jax.ShapeDtypeStruct((8, *level_one.shape), level_one.dtype),
+            jax.ShapeDtypeStruct((32, level_two.shape[0], *level_two.shape[2:]), level_two.dtype),
+            jax.ShapeDtypeStruct(tokens.shape, tokens.dtype),
+        ),
+        in_specs=[whole] * 5,
+        out_specs=(pl.BlockSpec(memory_space=pl.ANY), whole, whole, whole),
+        scratch_shapes=[dma((3,)), dma((7,)), dma((7,)), dma((39,)), dma((39,))],
         compiler_params=pltpu.CompilerParams(collective_id=3, has_side_effects=True),
         name="gather_z",
-    )(weight)
-
-
-GATHER_COST = pl.CostEstimate(flops=10**9, bytes_accessed=2**24, transcendentals=0)
-
-
-def gather_first(gathered, level_one, level_two, width):
-    whole = pl.BlockSpec(memory_space=pltpu.VMEM)
-    anywhere = pl.BlockSpec(memory_space=pl.ANY)
-    dma = pltpu.SemaphoreType.DMA
-    return pl.pallas_call(
-        functools.partial(gather_kernel, 0, width, True),
-        out_shape=(
-            jax.ShapeDtypeStruct(gathered.shape, gathered.dtype),
-            jax.ShapeDtypeStruct((8, *level_one.shape), level_one.dtype),
-            jax.ShapeDtypeStruct((32, level_two.shape[0], *level_two.shape[2:]), level_two.dtype),
-        ),
-        in_specs=[anywhere, whole, whole],
-        out_specs=(anywhere, whole, whole),
-        input_output_aliases={0: 0},
-        scratch_shapes=[
-            dma((GATHER_COPIES,)), dma((GATHER_COPIES,)), dma((2,)), dma((39,)), dma((39,)),
-        ],
-        compiler_params=pltpu.CompilerParams(collective_id=0, has_side_effects=True),
-        cost_estimate=GATHER_COST,
-        name="gather_first",
-    )(gathered, level_one, level_two)
-
-
-def gather_rest(gathered, low):
+    )(weight, level_one, level_two, tokens, gain)
+
+
+def gather_xy(gathered, low, width, collective_id):
     dma = pltpu.SemaphoreType.DMA
     anywhere = pl.BlockSpec(memory_space=pl.ANY)
     return pl.pallas_call(
-        functools.partial(gather_kernel, low, gathered.shape[-1] - low, False),
+        functools.partial(gather_kernel, low, width),
         out_shape=jax.ShapeDtypeStruct(gathered.shape, gathered.dtype),
         in_specs=[anywhere],
         out_specs=anywhere,
         input_output_aliases={0: 0},
         scratch_shapes=[dma((GATHER_COPIES,)), dma((GATHER_COPIES,))],
-        compiler_params=pltpu.CompilerParams(collective_id=1, has_side_effects=True),
-        cost_estimate=GATHER_COST,
-        name="gather_rest",
+        compiler_params=pltpu.CompilerParams(collective_id=collective_id, has_side_effects=True),
+        cost_estimate=pl.CostEstimate(flops=10**9, bytes_accessed=2**24, transcendentals=0),
+        name="gather_xy",
     )(gathered)
 
 
@@ -524,17 +510,18 @@
     after = lax.optimization_barrier
 
     tokens_float = tokens.astype(jnp.float32)
-    inverse_rms = lax.rsqrt(jnp.mean(tokens_float * tokens_float, axis=3, keepdims=True) + EPSILON)
-    normed = (tokens_float * inverse_rms * norm_gain).astype(jnp.bfloat16)
-
-    parts, gathered = after((pack_blocks(normed), gather_z(gate_weight)))
-    normed_block = exchange(parts)
-    gathered, block_one, block_two = gather_first(
-        gathered,
+    gathered, block_one, block_two, normed = gather_z(
+        gate_weight,
         level_one.reshape(own_j, -1, 128),
         level_two.reshape(own_i, level_two.shape[1], -1, 128),
-        channels // 2,
-    )
+        tokens,
+        norm_gain.reshape(1, -1),
+    )
+    parts, gathered, block_one, block_two = after(
+        (pack_blocks(normed), gathered, block_one, block_two)
+    )
+    normed_block = exchange(parts)
+    gathered = gather_xy(gathered, 0, channels // 2, 0)
     block_one = block_one.reshape(sb, own_j * m1, m1)
     block_two = block_two.reshape(8, -1, m2)
     wide = (8, 256, 256)
@@ -547,7 +534,7 @@
     )
     parts, gathered = after((second_mix.reshape(parts.shape), gathered))
     second_mix = exchange(parts)
-    gathered = gather_rest(gathered, channels // 2).reshape(-1, channels)
+    gathered = gather_xy(gathered, channels // 2, channels // 2, 1).reshape(-1, channels)
     gate_pre = dot("tr,rc->tc", normed.reshape(-1, channels), gathered).reshape(tokens.shape)
     gate_pre, second_mix = after((gate_pre, second_mix))
     second_mix = unpack_tokens(second_mix, own_i, own_j)
@@ -563,11 +550,17 @@
     ).astype(jnp.bfloat16)
     grad_second = dot("ijok,ijoc->ijkc", level_three, grad_mixed).astype(jnp.bfloat16)
 
-    parts, grad_gate, grad_mixed = after((pack_blocks(grad_second), grad_gate, grad_mixed))
+    parts, grad_gate, grad_mixed, tokens_late = after(
+        (pack_blocks(grad_second), grad_gate, grad_mixed, tokens)
+    )
     grad_block = exchange(parts)
     back_term = dot("tc,rc->tr", grad_gate.reshape(-1, channels), gathered)
     grad_three = dot("ijoc,ijkc->ijok", grad_mixed, second_mix) * grad_scale
-    grad_block, back_term, grad_three = after((grad_block, back_term, grad_three))
+    tokens_late = tokens_late.astype(jnp.float32)
+    inverse_rms = lax.rsqrt(jnp.mean(tokens_late * tokens_late, axis=3, keepdims=True) + EPSILON)
+    grad_block, back_term, grad_three, inverse_rms = after(
+        (grad_block, back_term, grad_three, inverse_rms)
+    )
 
     grad_block = grad_block.reshape(grid)
     grad_first, grad_normed = local_call(

time: 254 us -> 255 us (level)
  other arithmetic: 6.99 us -> 4.2 us
  starting transfers between devices: 41.6 us -> 44.2 us
    all_to_all x4, starting transfers between devices: 41.6 us -> 44.2 us  [exchange(): return lax.all_to_all(parts, ALL, split_axis=0, concat_axis=0, tiled=True)]
  transfers between devices with their start and end apart: 4 -> 4, of which waited for: 1 -> 1; matrix products, arithmetic and copies ran while one was open for 10% -> 9% of each run, Pallas kernels for 47% -> 41%
where the time goes in v3:
time: 255 us; the launch traced here: 254 us
  Pallas kernels  140 us (55%)
  starting transfers between devices  44.2 us (17%)
  local copies, waits for them, and re-layouts  23.1 us (9%)
  waiting for transfers between devices  21.2 us (8%)
  matrix products  20.6 us (8%)
  other arithmetic  4.2 us (2%)
    pallas_call x2, Pallas kernels, gather_xy(): pl.pallas_call(functools.partial(gather_kernel, low, width), out_shape=ja...  64 us
    all_to_all x4, starting transfers between devices, exchange(): return lax.all_to_all(parts, ALL, split_axis=0, concat_axis=0, tiled=True)  44.2 us
    pallas_call x1, Pallas kernels, gather_z(): pl.pallas_call(gather_z_kernel, out_shape=(jax.ShapeDtypeStruct((4, 4, 2,...  28.9 us
    pallas_call x1, Pallas kernels, reduce_parts(): pl.pallas_call(functools.partial(reduce_kernel, scale), out_shape=(jax.Sh...  28.7 us
    all_to_all x4, waiting for transfers between devices, exchange(): return lax.all_to_all(parts, ALL, split_axis=0, concat_axis=0, tiled=True)  21.2 us
    dot_general x5, matrix products, dot(): return jnp.einsum(pattern, left, right, preferred_element_type=jnp.float32)  20.6 us
    pallas_call x4, Pallas kernels, local_call(): pl.pallas_call(kernel, out_shape=tuple((jax.ShapeDtypeStruct(shape, jnp.b...  18.5 us
  transfers between devices with their start and end apart: 4, of which 1 were waited for; matrix products, arithmetic and copies ran while one was open for 9% of the time, Pallas kernels for 41%

profile of v3, /device:TPU:9, one launch (start us, length us, event | category | flops | bytes accessed | tf_op | source)
XLA Modules:
  0.0 254.2 jit_solution(4860666608524150431)
XLA Ops:
  0.6 1.6 reshape.113.two_ref
  3.8 28.9 %gather_z.1 = (bf16[4,4,2,2,4,8,2048]{6,5,4,3,2,1,0:T(8,128)(2,1)}, bf16[8,4,32,128]{3,2,1,0:T(8,128)(2,1)}, bf16[32,2,8,128]{3,2,1,0:T(8,128)(2,1)}, bf16[2,4,32,2048]{3,2,1,0:T(8,128)(2,1)}) custom-call(bf16[8,2048]{1,0:T(8,128)(2,1)} %w_ref.1, bf16[4,32,128]{2,1,0:T(8,128)(2,1)} %reshape.112.one_ref, bf16[2,4,8,128]{3,2,1,0:T(8,128)(2,1)} %reshape.113.two_ref, ...), custom_call_target="tpu_custom_call" | custom-call | tf_op jit(solution)/shard_map/gather_z/pallas_call | solution.py:258
  35.8 13.2 %all-to-all-start = ((bf16[256,8,256]{2,1,0:T(8,128)(2,1)}), bf16[256,8,256]{2,1,0:T(8,128)(2,1)S(1)}, u32[]{:S(2)}, u32[]{:S(2)}) async-start(bf16[256,8,256]{2,1,0:T(8,128)(2,1)} %copy.30), calls=%async_computation | async-start | bytes 2097152 | tf_op jit(solution)/shard_map/all_to_all | solution.py:32
  51.1 31.2 %gather_xy.2._ = bf16[4,4,2,2,4,8,2048]{6,5,4,3,2,1,0:T(8,128)(2,1)} custom-call(bf16[4,4,2,2,4,8,2048]{6,5,4,3,2,1,0:T(8,128)(2,1)} %get-tuple-element.51._), custom_call_target="tpu_custom_call", output_to_operand_aliasing={{}: (0, {})} | custom-call | flops 1000000000 | bytes 16777216 | tf_op jit(solution)/shard_map/gather_xy/pallas_call | solution.py:277
  82.3 3.8 %widen_kernel.1 = (bf16[8,256,256]{2,1,0:T(8,128)(2,1)}, bf16[8,256,256]{2,1,0:T(8,128)(2,1)}) custom-call(bf16[8,256,64]{2,1,0:T(8,128)(2,1)} %reshape.118.one_ref, bf16[8,256,32]{2,1,0:T(8,128)(2,1)} %reshape.119.two_ref), custom_call_target="tpu_custom_call" | custom-call | flops 1000000000 | bytes 4194304 | tf_op jit(solution)/shard_map/widen_kernel/pallas_call | solution.py:491
  87.0 3.6 %forward_kernel.1 = (bf16[32,8,8,256]{3,2,1,0:T(8,128)(2,1)}, bf16[32,8,8,256]{3,2,1,0:T(8,128)(2,1)}) custom-call(bf16[32,8,8,256]{3,2,1,0:T(8,128)(2,1)} %bitcast.81, bf16[8,256,256]{2,1,0:T(8,128)(2,1)} %get-tuple-element.48.wide_one, bf16[8,256,256]{2,1,0:T(8,128)(2,1)} %get-tuple-element.49.wide_two), custom_call_target="tpu_custom_call" | custom-call | flops 1000000000 | bytes 4194304 | tf_op jit(solution)/shard_map/forward_kernel/pallas_call | solution.py:491
  90.7 11.5 %all-to-all-start.1 = ((bf16[256,8,256]{2,1,0:T(8,128)(2,1)}), bf16[256,8,256]{2,1,0:T(8,128)(2,1)S(1)}, u32[]{:S(2)}, u32[]{:S(2)}) async-start(bf16[256,8,256]{2,1,0:T(8,128)(2,1)} %bitcast.85), calls=%async_computation.1 | async-start | bytes 2097152 | tf_op jit(solution)/shard_map/all_to_all | solution.py:32
  102.2 32.8 %gather_xy.3 = bf16[4,4,2,2,4,8,2048]{6,5,4,3,2,1,0:T(8,128)(2,1)} custom-call(bf16[4,4,2,2,4,8,2048]{6,5,4,3,2,1,0:T(8,128)(2,1)} %gather_xy.2._), custom_call_target="tpu_custom_call", output_to_operand_aliasing={{}: (0, {})} | custom-call | flops 1000000000 | bytes 16777216 | tf_op jit(solution)/shard_map/gather_xy/pallas_call | solution.py:277
  135.0 7.0 %fusion.11 = f32[2,4,32,2048]{3,2,1,0:T(8,128)} fusion(bf16[2,4,32,2048]{3,2,1,0:T(8,128)(2,1)S(1)} %copy-done.5, bf16[2048,2048,1,1]{1,0,3,2:T(8,128)(2,1)} %bitcast.73), kind=kOutput, calls=%fused_computation.26 | convolution fusion | flops 2147483648 | bytes 11534336 | tf_op jit(solution)/shard_map/tr,rc->tc/dot_general | solution.py:502
  143.2 4.9 %fusion.8 = (bf16[2,4,32,2048]{3,2,1,0:T(8,128)(2,1)}, bf16[2,4,32,2048]{3,2,1,0:T(8,128)(2,1)}, bf16[2,4,32,2048]{3,2,1,0:T(8,128)(2,1)S(1)}) fusion(bf16[2,4,32,2048]{3,2,1,0:T(8,128)(2,1)} %param.13, f32[2,4,32,2048]{3,2,1,0:T(8,128)} %fusion.11, bf16[2,4,32,2048]{3,2,1,0:T(8,128)(2,1)S(1)} %copy-done.1, bf16[2,4,32,32]{3,2,1,0:T(8,128)(2,1)S(1)} %copy-done, ...), kind=kOutput, calls=%fused_computation.16 | convolution fusion | flops 42991616 | bytes 8404992 | tf_op jit(solution)/shard_map/ijok,ijkc->ijoc/dot_general | solution.py:502
  148.9 1.6 copy.32
  150.5 12.1 %all-to-all-start.2 = ((bf16[256,8,256]{2,1,0:T(8,128)(2,1)}), bf16[256,8,256]{2,1,0:T(8,128)(2,1)}, u32[]{:S(2)}, u32[]{:S(2)}) async-start(bf16[256,8,256]{2,1,0:T(8,128)(2,1)} %copy.32), calls=%async_computation.2 | async-start | bytes 2097152 | tf_op jit(solution)/shard_map/all_to_all | solution.py:32
  164.0 7.1 %fusion.12 = f32[256,2048]{1,0:T(8,128)} fusion(bf16[256,2048]{1,0:T(8,128)(2,1)S(1)} %bitcast.90, bf16[2048,2048]{1,0:T(8,128)(2,1)} %bitcast.74), kind=kOutput, calls=%fused_computation.27 | convolution fusion | flops 2147483648 | bytes 11534336 | tf_op jit(solution)/shard_map/tc,rc->tr/dot_general | solution.py:502
  171.1 21.2 %all-to-all-done.2 = bf16[256,8,256]{2,1,0:T(8,128)(2,1)} async-done(((bf16[256,8,256]{2,1,0:T(8,128)(2,1)}), bf16[256,8,256]{2,1,0:T(8,128)(2,1)}, u32[]{:S(2)}, u32[]{:S(2)}) %all-to-all-start.2) | async-done | bytes 1048608 | tf_op jit(solution)/shard_map/all_to_all | solution.py:32
  192.3 3.7 %backward_kernel.1 = (bf16[32,8,8,256]{3,2,1,0:T(8,128)(2,1)}, bf16[32,8,8,256]{3,2,1,0:T(8,128)(2,1)}) custom-call(bf16[32,8,8,256]{3,2,1,0:T(8,128)(2,1)} %bitcast.17.got.grad_second, bf16[8,256,256]{2,1,0:T(8,128)(2,1)} %get-tuple-element.48.wide_one, bf16[8,256,256]{2,1,0:T(8,128)(2,1)} %get-tuple-element.49.wide_two), custom_call_target="tpu_custom_call" | custom-call | flops 1000000000 | bytes 4194304 | tf_op jit(solution)/shard_map/backward_kernel/pallas_call | solution.py:491
  196.0 7.5 %all-to-all-start.3 = ((bf16[256,8,256]{2,1,0:T(8,128)(2,1)}), bf16[256,8,256]{2,1,0:T(8,128)(2,1)S(1)}, u32[]{:S(2)}, u32[]{:S(2)}) async-start(bf16[256,8,256]{2,1,0:T(8,128)(2,1)} %bitcast.84), calls=%async_computation.3 | async-start | bytes 2097152 | tf_op jit(solution)/shard_map/all_to_all | solution.py:32
  203.5 7.4 %parts_kernel.1 = (bf16[8,256,64]{2,1,0:T(8,128)(2,1)}, bf16[8,256,32]{2,1,0:T(8,128)(2,1)}) custom-call(bf16[32,8,8,256]{3,2,1,0:T(8,128)(2,1)} %bitcast.17.got.grad_second, bf16[32,8,8,256]{3,2,1,0:T(8,128)(2,1)} %get-tuple-element.66.first_mix, bf16[32,8,8,256]{3,2,1,0:T(8,128)(2,1)} %get-tuple-element.67.grad_first, bf16[32,8,8,256]{3,2,1,0:T(8,128)(2,1)} %bitcast.82), custom_call_target="tpu_custom_call" | custom-call | flops 1000000000 | bytes 4194304 | tf_op jit(solution)/shard_map/parts_kernel/pallas_call | solution.py:491
  210.9 2.0 reshape.129.one_ref
  212.9 2.0 reshape.130.two_ref
  214.9 28.7 %reduce_parts.1 = (f32[128,128]{1,0:T(8,128)}, f32[4,2,8,128]{3,2,1,0:T(8,128)}) custom-call(bf16[8,128,128]{2,1,0:T(8,128)(2,1)} %reshape.129.one_ref, bf16[32,2,8,128]{3,2,1,0:T(8,128)(2,1)} %reshape.130.two_ref), custom_call_target="tpu_custom_call" | custom-call | flops 100000000 | bytes 1048576 | tf_op jit(solution)/shard_map/reduce_parts/pallas_call | solution.py:379
  243.6 1.6 reshape.132
  248.3 1.7 reshape.134
  250.0 2.2 fusion.4
  252.5 1.7 fusion.3
  (40 shorter events, 14.4 us)
Async XLA Ops:
  0.6 142.1 %copy-start = (bf16[2,4,32,32]{3,2,1,0:T(8,128)(2,1)S(1)}, bf16[2,4,32,32]{3,2,1,0:T(8,128)(2,1)}, u32[]{:S(2)}) copy-start(bf16[2,4,32,32]{3,2,1,0:T(8,128)(2,1)} %param.12) | copy-start | bytes 49156
  34.3 14.7 %copy-start.6 = (bf16[8,4,32,128]{3,2,1,0:T(8,128)(2,1)S(1)}, bf16[8,4,32,128]{3,2,1,0:T(8,128)(2,1)}, u32[]{:S(2)}) copy-start(bf16[8,4,32,128]{3,2,1,0:T(8,128)(2,1)} %get-tuple-element.46) | copy-start | bytes 786436
  34.3 15.8 %copy-start.7 = (bf16[32,2,8,128]{3,2,1,0:T(8,128)(2,1)S(1)}, bf16[32,2,8,128]{3,2,1,0:T(8,128)(2,1)}, u32[]{:S(2)}) copy-start(bf16[32,2,8,128]{3,2,1,0:T(8,128)(2,1)} %get-tuple-element.47) | copy-start | bytes 393220
  35.8 50.2 %all-to-all-start = ((bf16[256,8,256]{2,1,0:T(8,128)(2,1)}), bf16[256,8,256]{2,1,0:T(8,128)(2,1)S(1)}, u32[]{:S(2)}, u32[]{:S(2)}) async-start(bf16[256,8,256]{2,1,0:T(8,128)(2,1)} %copy.30), calls=%async_computation | async-start | bytes 2097152 | tf_op jit(solution)/shard_map/all_to_all | solution.py:32
  86.1 1.0 copy-start.3
  90.7 51.4 %all-to-all-start.1 = ((bf16[256,8,256]{2,1,0:T(8,128)(2,1)}), bf16[256,8,256]{2,1,0:T(8,128)(2,1)S(1)}, u32[]{:S(2)}, u32[]{:S(2)}) async-start(bf16[256,8,256]{2,1,0:T(8,128)(2,1)} %bitcast.85), calls=%async_computation.1 | async-start | bytes 2097152 | tf_op jit(solution)/shard_map/all_to_all | solution.py:32
  102.2 32.8 %copy-start.5 = (bf16[2,4,32,2048]{3,2,1,0:T(8,128)(2,1)S(1)}, bf16[2,4,32,2048]{3,2,1,0:T(8,128)(2,1)}, u32[]{:S(2)}) copy-start(bf16[2,4,32,2048]{3,2,1,0:T(8,128)(2,1)} %get-tuple-element.41) | copy-start | bytes 3145732
  142.0 1.2 copy-start.1
  150.5 41.8 %all-to-all-start.2 = ((bf16[256,8,256]{2,1,0:T(8,128)(2,1)}), bf16[256,8,256]{2,1,0:T(8,128)(2,1)}, u32[]{:S(2)}, u32[]{:S(2)}) async-start(bf16[256,8,256]{2,1,0:T(8,128)(2,1)} %copy.32), calls=%async_computation.2 | async-start | bytes 2097152 | tf_op jit(solution)/shard_map/all_to_all | solution.py:32
  162.6 1.4 copy-start.9
  196.0 47.6 %all-to-all-start.3 = ((bf16[256,8,256]{2,1,0:T(8,128)(2,1)}), bf16[256,8,256]{2,1,0:T(8,128)(2,1)S(1)}, u32[]{:S(2)}, u32[]{:S(2)}) async-start(bf16[256,8,256]{2,1,0:T(8,128)(2,1)} %bitcast.84), calls=%async_computation.3 | async-start | bytes 2097152 | tf_op jit(solution)/shard_map/all_to_all | solution.py:32
  248.3 1.7 copy-start.8
  250.0 2.2 copy-start.2
  250.0 2.5 copy-start.4

commit v4 on v3

--- a/solution.py
+++ b/solution.py
@@ -536,30 +536,27 @@
     second_mix = exchange(parts)
     gathered = gather_xy(gathered, channels // 2, channels // 2, 1).reshape(-1, channels)
     gate_pre = dot("tr,rc->tc", normed.reshape(-1, channels), gathered).reshape(tokens.shape)
-    gate_pre, second_mix = after((gate_pre, second_mix))
+    upstream_float = upstream.astype(jnp.float32)
+    grad_mixed = (upstream_float * (gate_pre * jax.nn.sigmoid(gate_pre))).astype(jnp.bfloat16)
+    grad_second = dot("ijok,ijoc->ijkc", level_three, grad_mixed).astype(jnp.bfloat16)
+    parts, second_mix, gate_pre, tokens_late = after(
+        (pack_blocks(grad_second), second_mix, gate_pre, tokens)
+    )
+    grad_block = exchange(parts)
+
     second_mix = unpack_tokens(second_mix, own_i, own_j)
     mixed_all = dot("ijok,ijkc->ijoc", level_three, second_mix)
-
     gate_sigmoid = jax.nn.sigmoid(gate_pre)
-    gate_value = gate_pre * gate_sigmoid
-    output = (tokens_float + mixed_all * gate_value).astype(jnp.bfloat16)
-    upstream_float = upstream.astype(jnp.float32)
-    grad_mixed = (upstream_float * gate_value).astype(jnp.bfloat16)
+    output = (tokens_float + mixed_all * (gate_pre * gate_sigmoid)).astype(jnp.bfloat16)
     grad_gate = (
         upstream_float * mixed_all * gate_sigmoid * (1.0 + gate_pre * (1.0 - gate_sigmoid))
     ).astype(jnp.bfloat16)
-    grad_second = dot("ijok,ijoc->ijkc", level_three, grad_mixed).astype(jnp.bfloat16)
-
-    parts, grad_gate, grad_mixed, tokens_late = after(
-        (pack_blocks(grad_second), grad_gate, grad_mixed, tokens)
-    )
-    grad_block = exchange(parts)
     back_term = dot("tc,rc->tr", grad_gate.reshape(-1, channels), gathered)
     grad_three = dot("ijoc,ijkc->ijok", grad_mixed, second_mix) * grad_scale
     tokens_late = tokens_late.astype(jnp.float32)
     inverse_rms = lax.rsqrt(jnp.mean(tokens_late * tokens_late, axis=3, keepdims=True) + EPSILON)
-    grad_block, back_term, grad_three, inverse_rms = after(
-        (grad_block, back_term, grad_three, inverse_rms)
+    grad_block, back_term, grad_three, inverse_rms, output = after(
+        (grad_block, back_term, grad_three, inverse_rms, output)
     )
 
     grad_block = grad_block.reshape(grid)

time: 255 us -> 250 us (0.980)
  matrix products: 20.6 us -> 15.3 us
    dot_general x5, matrix products: 20.6 us -> 15.3 us  [dot(): return jnp.einsum(pattern, left, right, preferred_element_type=jnp.float32)]
  transfers between devices with their start and end apart: 4 -> 4, of which waited for: 1 -> 1; matrix products, arithmetic and copies ran while one was open for 9% -> 11% of each run, Pallas kernels for 41% -> 42%
where the time goes in v4:
time: 250 us; the launch traced here: 249 us
  Pallas kernels  140 us (56%)
  starting transfers between devices  44.3 us (18%)
  local copies, waits for them, and re-layouts  25.5 us (10%)
  waiting for transfers between devices  18.7 us (7%)
  matrix products  15.3 us (6%)
  other arithmetic  4.2 us (2%)
    pallas_call x2, Pallas kernels, gather_xy(): pl.pallas_call(functools.partial(gather_kernel, low, width), out_shape=ja...  63.8 us
    all_to_all x4, starting transfers between devices, exchange(): return lax.all_to_all(parts, ALL, split_axis=0, concat_axis=0, tiled=True)  44.3 us
    pallas_call x1, Pallas kernels, gather_z(): pl.pallas_call(gather_z_kernel, out_shape=(jax.ShapeDtypeStruct((4, 4, 2,...  28.9 us
    pallas_call x1, Pallas kernels, reduce_parts(): pl.pallas_call(functools.partial(reduce_kernel, scale), out_shape=(jax.Sh...  28.7 us
    all_to_all x4, waiting for transfers between devices, exchange(): return lax.all_to_all(parts, ALL, split_axis=0, concat_axis=0, tiled=True)  18.7 us
    pallas_call x4, Pallas kernels, local_call(): pl.pallas_call(kernel, out_shape=tuple((jax.ShapeDtypeStruct(shape, jnp.b...  18.5 us
    dot_general x5, matrix products, dot(): return jnp.einsum(pattern, left, right, preferred_element_type=jnp.float32)  15.3 us
  transfers between devices with their start and end apart: 4, of which 1 were waited for; matrix products, arithmetic and copies ran while one was open for 11% of the time, Pallas kernels for 42%

profile of v4, /device:TPU:9, one launch (start us, length us, event | category | flops | bytes accessed | tf_op | source)
XLA Modules:
  0.0 248.7 jit_solution(11164957567187162560)
XLA Ops:
  0.6 1.6 reshape.113.two_ref
  3.8 28.9 %gather_z.1 = (bf16[4,4,2,2,4,8,2048]{6,5,4,3,2,1,0:T(8,128)(2,1)}, bf16[8,4,32,128]{3,2,1,0:T(8,128)(2,1)}, bf16[32,2,8,128]{3,2,1,0:T(8,128)(2,1)}, bf16[2,4,32,2048]{3,2,1,0:T(8,128)(2,1)}) custom-call(bf16[8,2048]{1,0:T(8,128)(2,1)} %w_ref.1, bf16[4,32,128]{2,1,0:T(8,128)(2,1)} %reshape.112.one_ref, bf16[2,4,8,128]{3,2,1,0:T(8,128)(2,1)} %reshape.113.two_ref, ...), custom_call_target="tpu_custom_call" | custom-call | tf_op jit(solution)/shard_map/gather_z/pallas_call | solution.py:258
  35.8 13.2 %all-to-all-start = ((bf16[256,8,256]{2,1,0:T(8,128)(2,1)}), bf16[256,8,256]{2,1,0:T(8,128)(2,1)S(1)}, u32[]{:S(2)}, u32[]{:S(2)}) async-start(bf16[256,8,256]{2,1,0:T(8,128)(2,1)} %copy.30), calls=%async_computation | async-start | bytes 2097152 | tf_op jit(solution)/shard_map/all_to_all | solution.py:32
  51.1 30.9 %gather_xy.2._ = bf16[4,4,2,2,4,8,2048]{6,5,4,3,2,1,0:T(8,128)(2,1)} custom-call(bf16[4,4,2,2,4,8,2048]{6,5,4,3,2,1,0:T(8,128)(2,1)} %get-tuple-element.50._), custom_call_target="tpu_custom_call", output_to_operand_aliasing={{}: (0, {})} | custom-call | flops 1000000000 | bytes 16777216 | tf_op jit(solution)/shard_map/gather_xy/pallas_call | solution.py:277
  82.1 3.8 %widen_kernel.1 = (bf16[8,256,256]{2,1,0:T(8,128)(2,1)}, bf16[8,256,256]{2,1,0:T(8,128)(2,1)}) custom-call(bf16[8,256,64]{2,1,0:T(8,128)(2,1)} %reshape.118.one_ref, bf16[8,256,32]{2,1,0:T(8,128)(2,1)} %reshape.119.two_ref), custom_call_target="tpu_custom_call" | custom-call | flops 1000000000 | bytes 4194304 | tf_op jit(solution)/shard_map/widen_kernel/pallas_call | solution.py:491
  86.8 3.6 %forward_kernel.1 = (bf16[32,8,8,256]{3,2,1,0:T(8,128)(2,1)}, bf16[32,8,8,256]{3,2,1,0:T(8,128)(2,1)}) custom-call(bf16[32,8,8,256]{3,2,1,0:T(8,128)(2,1)} %bitcast.83, bf16[8,256,256]{2,1,0:T(8,128)(2,1)} %get-tuple-element.47.wide_one, bf16[8,256,256]{2,1,0:T(8,128)(2,1)} %get-tuple-element.48.wide_two), custom_call_target="tpu_custom_call" | custom-call | flops 1000000000 | bytes 4194304 | tf_op jit(solution)/shard_map/forward_kernel/pallas_call | solution.py:491
  90.5 11.6 %all-to-all-start.1 = ((bf16[256,8,256]{2,1,0:T(8,128)(2,1)}), bf16[256,8,256]{2,1,0:T(8,128)(2,1)S(1)}, u32[]{:S(2)}, u32[]{:S(2)}) async-start(bf16[256,8,256]{2,1,0:T(8,128)(2,1)} %bitcast.87), calls=%async_computation.1 | async-start | bytes 2097152 | tf_op jit(solution)/shard_map/all_to_all | solution.py:32
  102.1 32.8 %gather_xy.3 = bf16[4,4,2,2,4,8,2048]{6,5,4,3,2,1,0:T(8,128)(2,1)} custom-call(bf16[4,4,2,2,4,8,2048]{6,5,4,3,2,1,0:T(8,128)(2,1)} %gather_xy.2._), custom_call_target="tpu_custom_call", output_to_operand_aliasing={{}: (0, {})} | custom-call | flops 1000000000 | bytes 16777216 | tf_op jit(solution)/shard_map/gather_xy/pallas_call | solution.py:277
  135.0 7.7 %fusion = (bf16[2,4,32,2048]{3,2,1,0:T(8,128)(2,1)S(1)}, f32[2,4,32,2048]{3,2,1,0:T(8,128)}) fusion(bf16[2,4,32,2048]{3,2,1,0:T(8,128)(2,1)S(1)} %copy-done.4, bf16[2,4,32,2048]{3,2,1,0:T(8,128)(2,1)} %get-tuple-element.40, bf16[2048,2048,1,1]{1,0,3,2:T(8,128)(2,1)} %bitcast.73), kind=kOutput, calls=%fused_computation.8 | convolution fusion | flops 2151153664 | bytes 13631488 | tf_op jit(solution)/shard_map/tr,rc->tc/dot_general | solution.py:502
  143.4 1.6 copy.31
  145.0 12.1 %all-to-all-start.2 = ((bf16[256,8,256]{2,1,0:T(8,128)(2,1)}), bf16[256,8,256]{2,1,0:T(8,128)(2,1)}, u32[]{:S(2)}, u32[]{:S(2)}) async-start(bf16[256,8,256]{2,1,0:T(8,128)(2,1)} %copy.31), calls=%async_computation.2 | async-start | bytes 2097152 | tf_op jit(solution)/shard_map/all_to_all | solution.py:32
  161.8 2.4 fusion.6
  164.4 3.7 %fusion.10 = f32[256,2048]{1,0:T(8,128)} fusion(bf16[256,2048]{1,0:T(8,128)(2,1)S(1)} %bitcast.92, bf16[2048,2048]{1,0:T(8,128)(2,1)S(1)} %bitcast.76), kind=kOutput, calls=%fused_computation.25 | convolution fusion | flops 2147483648 | bytes 11534336 | tf_op jit(solution)/shard_map/tc,rc->tr/dot_general | solution.py:502
  168.1 18.6 %all-to-all-done.2 = bf16[256,8,256]{2,1,0:T(8,128)(2,1)} async-done(((bf16[256,8,256]{2,1,0:T(8,128)(2,1)}), bf16[256,8,256]{2,1,0:T(8,128)(2,1)}, u32[]{:S(2)}, u32[]{:S(2)}) %all-to-all-start.2) | async-done | bytes 1048608 | tf_op jit(solution)/shard_map/all_to_all | solution.py:32
  186.8 3.7 %backward_kernel.1 = (bf16[32,8,8,256]{3,2,1,0:T(8,128)(2,1)}, bf16[32,8,8,256]{3,2,1,0:T(8,128)(2,1)}) custom-call(bf16[32,8,8,256]{3,2,1,0:T(8,128)(2,1)} %bitcast.17.got.grad_second, bf16[8,256,256]{2,1,0:T(8,128)(2,1)} %get-tuple-element.47.wide_one, bf16[8,256,256]{2,1,0:T(8,128)(2,1)} %get-tuple-element.48.wide_two), custom_call_target="tpu_custom_call" | custom-call | flops 1000000000 | bytes 4194304 | tf_op jit(solution)/shard_map/backward_kernel/pallas_call | solution.py:491
  190.5 7.5 %all-to-all-start.3 = ((bf16[256,8,256]{2,1,0:T(8,128)(2,1)}), bf16[256,8,256]{2,1,0:T(8,128)(2,1)S(1)}, u32[]{:S(2)}, u32[]{:S(2)}) async-start(bf16[256,8,256]{2,1,0:T(8,128)(2,1)} %bitcast.86), calls=%async_computation.3 | async-start | bytes 2097152 | tf_op jit(solution)/shard_map/all_to_all | solution.py:32
  198.0 7.4 %parts_kernel.1 = (bf16[8,256,64]{2,1,0:T(8,128)(2,1)}, bf16[8,256,32]{2,1,0:T(8,128)(2,1)}) custom-call(bf16[32,8,8,256]{3,2,1,0:T(8,128)(2,1)} %bitcast.17.got.grad_second, bf16[32,8,8,256]{3,2,1,0:T(8,128)(2,1)} %get-tuple-element.64.first_mix, bf16[32,8,8,256]{3,2,1,0:T(8,128)(2,1)} %get-tuple-element.65.grad_first, bf16[32,8,8,256]{3,2,1,0:T(8,128)(2,1)} %bitcast.84), custom_call_target="tpu_custom_call" | custom-call | flops 1000000000 | bytes 4194304 | tf_op jit(solution)/shard_map/parts_kernel/pallas_call | solution.py:491
  205.4 2.0 reshape.129.one_ref
  207.4 2.0 reshape.130.two_ref
  209.4 28.7 %reduce_parts.1 = (f32[128,128]{1,0:T(8,128)}, f32[4,2,8,128]{3,2,1,0:T(8,128)}) custom-call(bf16[8,128,128]{2,1,0:T(8,128)(2,1)} %reshape.129.one_ref, bf16[32,2,8,128]{3,2,1,0:T(8,128)(2,1)} %reshape.130.two_ref), custom_call_target="tpu_custom_call" | custom-call | flops 100000000 | bytes 1048576 | tf_op jit(solution)/shard_map/reduce_parts/pallas_call | solution.py:379
  238.1 1.6 reshape.132
  242.7 1.7 reshape.134
  244.5 2.2 fusion.8
  247.0 1.7 fusion.5
  (47 shorter events, 16.8 us)
Async XLA Ops:
  0.6 142.0 %copy-start = (bf16[2,4,32,32]{3,2,1,0:T(8,128)(2,1)S(1)}, bf16[2,4,32,32]{3,2,1,0:T(8,128)(2,1)}, u32[]{:S(2)}) copy-start(bf16[2,4,32,32]{3,2,1,0:T(8,128)(2,1)} %param.12) | copy-start | bytes 49156
  34.2 14.7 %copy-start.7 = (bf16[8,4,32,128]{3,2,1,0:T(8,128)(2,1)S(1)}, bf16[8,4,32,128]{3,2,1,0:T(8,128)(2,1)}, u32[]{:S(2)}) copy-start(bf16[8,4,32,128]{3,2,1,0:T(8,128)(2,1)} %get-tuple-element.45) | copy-start | bytes 786436
  34.2 15.8 %copy-start.8 = (bf16[32,2,8,128]{3,2,1,0:T(8,128)(2,1)S(1)}, bf16[32,2,8,128]{3,2,1,0:T(8,128)(2,1)}, u32[]{:S(2)}) copy-start(bf16[32,2,8,128]{3,2,1,0:T(8,128)(2,1)} %get-tuple-element.46) | copy-start | bytes 393220
  35.8 50.1 %all-to-all-start = ((bf16[256,8,256]{2,1,0:T(8,128)(2,1)}), bf16[256,8,256]{2,1,0:T(8,128)(2,1)S(1)}, u32[]{:S(2)}, u32[]{:S(2)}) async-start(bf16[256,8,256]{2,1,0:T(8,128)(2,1)} %copy.30), calls=%async_computation | async-start | bytes 2097152 | tf_op jit(solution)/shard_map/all_to_all | solution.py:32
  85.9 1.0 copy-start.3
  90.5 54.5 %all-to-all-start.1 = ((bf16[256,8,256]{2,1,0:T(8,128)(2,1)}), bf16[256,8,256]{2,1,0:T(8,128)(2,1)S(1)}, u32[]{:S(2)}, u32[]{:S(2)}) async-start(bf16[256,8,256]{2,1,0:T(8,128)(2,1)} %bitcast.87), calls=%async_computation.1 | async-start | bytes 2097152 | tf_op jit(solution)/shard_map/all_to_all | solution.py:32
  102.1 32.8 %copy-start.4 = (bf16[2,4,32,2048]{3,2,1,0:T(8,128)(2,1)S(1)}, bf16[2,4,32,2048]{3,2,1,0:T(8,128)(2,1)}, u32[]{:S(2)}) copy-start(bf16[2,4,32,2048]{3,2,1,0:T(8,128)(2,1)} %param.13) | copy-start | bytes 3145732
  145.0 41.8 %all-to-all-start.2 = ((bf16[256,8,256]{2,1,0:T(8,128)(2,1)}), bf16[256,8,256]{2,1,0:T(8,128)(2,1)}, u32[]{:S(2)}, u32[]{:S(2)}) async-start(bf16[256,8,256]{2,1,0:T(8,128)(2,1)} %copy.31), calls=%async_computation.2 | async-start | bytes 2097152 | tf_op jit(solution)/shard_map/all_to_all | solution.py:32
  157.1 2.7 %copy-start.1 = (bf16[2,4,32,2048]{3,2,1,0:T(8,128)(2,1)S(1)}, bf16[2,4,32,2048]{3,2,1,0:T(8,128)(2,1)}, u32[]{:S(2)}) copy-start(bf16[2,4,32,2048]{3,2,1,0:T(8,128)(2,1)} %tokens_ref.1) | copy-start | bytes 3145732
  159.8 1.4 copy-start.5
  159.9 2.0 copy-start.10
  160.2 4.0 %slice-start = ((s8[8388608]{0:T(1024)(128)(4,1)}), s8[4194304]{0:T(1024)(128)(4,1)S(1)}, s32[]{:S(2)}) async-start(s8[8388608]{0:T(1024)(128)(4,1)} %bitcast.74), calls=%async_computation.4 | async-start | bytes 8388608
  161.8 2.6 %slice-start.1 = ((s8[8388608]{0:T(1024)(128)(4,1)}), s8[4194304]{0:T(1024)(128)(4,1)S(1)}, s32[]{:S(2)}) async-start(s8[8388608]{0:T(1024)(128)(4,1)} %bitcast.74), calls=%async_computation.5 | async-start | bytes 8388608
  190.5 47.6 %all-to-all-start.3 = ((bf16[256,8,256]{2,1,0:T(8,128)(2,1)}), bf16[256,8,256]{2,1,0:T(8,128)(2,1)S(1)}, u32[]{:S(2)}, u32[]{:S(2)}) async-start(bf16[256,8,256]{2,1,0:T(8,128)(2,1)} %bitcast.86), calls=%async_computation.3 | async-start | bytes 2097152 | tf_op jit(solution)/shard_map/all_to_all | solution.py:32
  242.7 1.7 copy-start.9
  244.5 2.2 copy-start.2
  244.5 2.5 copy-start.6
